TPU v7x, 256 devices: a whole 4x4x8 slice. The times are simulated.
256 devices in a mesh: gx: 8 (over z_lo, core), gy: 4 (over x), gz: 8 (over y, z_hi).
Axes of the slice: x: 4, y: 4, z: 8 (z_hi: 2, z_lo: 4; z = z_hi * 4 + z_lo), core: 2. Of those that a mesh axis runs over, the one named last changes fastest.
Arguments:
- displacement: float32 [3, 48, 24, 3072], P(None, 'gx', 'gy', 'gz'), may hold values from -0.18 to 0.18
- size_field_modes: float32 [27, 16, 8, 1024], P(None, 'gx', 'gy', 'gz'), may hold values from -6 to 6
- velocity: float32 [3, 16, 8, 1024], P(None, 'gx', 'gy', 'gz'), may hold values from -1 to 1
Outputs:
- advected_field: float32 [27, 16, 8, 1024], P(None, 'gx', 'gy', 'gz')
- gradient: float32 [3, 48, 24, 3072], P(None, 'gx', 'gy', 'gz')
- checks: float32 [3], replicated
All inputs are finite; a program needn't handle non-finite values. Where the computation divides by a largest or mean magnitude, that divisor is 1e-20 or more.
Results may differ from a plain program's by a relative error of at most 0.0001.
Values sent between devices are 32-bit elements; how exact they have to be, the bound alone decides.
A program may use at most 64 MiB of HBM per device.

v0:
```python
import jax
import jax.numpy as jnp
import numpy as np
from jax import lax
from jax.sharding import Mesh
from jax.sharding import PartitionSpec as P

SUBSTEPS = 4
GX = ("gx_0", "gx_1")
GZ = ("gz_0", "gz_1")
GX_GY_GZ = ("gx_0", "gx_1", "gy", "gz_0", "gz_1")


root_half = 0.7071067811865476
root_three_half = 1.224744871391589
root_five_half = 1.5811388300841898
plus_values = (0.7071067811865476, 1.224744871391589, 1.5811388300841898)
minus_values = (0.7071067811865476, -1.224744871391589, 1.5811388300841898)
stiffness = ((0.0, 0.0, 0.0), (1.7320508075688772, 0.0, 0.0), (0.0, 3.872983346207417, 0.0))
courant = 0.1
theta_size = 0.3
trial_step = 0.05


def passed_along(x, axis, by):
    count = lax.axis_size(axis)
    return lax.ppermute(x, axis, [(i, (i + by) % count) for i in range(count)])


def one_axis_at_a_time(x, axes):
    for axis in axes:
        x = lax.pmax(x, axis)
    return x


def with_halo(x, sides, width):
    edges = {}
    for axis, dim in sides:
        count, length = (lax.axis_size(axis), x.shape[dim])
        up = [(i, (i + 1) % count) for i in range(count)]
        last = lax.slice_in_dim(x, length - width, length, axis=dim)
        leading = lax.slice_in_dim(x, 0, width, axis=dim)
        edges[dim] = (
            lax.ppermute(last, axis, up),
            lax.ppermute(leading, axis, [(b, a) for a, b in up]),
        )
    done = []
    for _, dim in sides:
        low, high = edges[dim]
        around = [(width, width) if d in done else (0, 0) for d in range(x.ndim)]
        x = jnp.concatenate([jnp.pad(low, around), x, jnp.pad(high, around)], axis=dim)
        done.append(dim)
    return x


def one_axis_at_a_time_2(x, axes):
    for axis in axes:
        x = lax.psum(x, axis)
    return x


def build_tables():
    points = np.array(
        [-0.8611363115940526, -0.3399810435848563, 0.3399810435848563, 0.8611363115940526]
    )
    weights = np.array(
        [0.3478548451374538, 0.6521451548625461, 0.6521451548625461, 0.3478548451374538]
    )
    points = 0.5 * (points + 1.0)
    weights = 0.5 * weights
    node_points = np.array([0.0, 1.0 / 3.0, 2.0 / 3.0, 1.0])
    value_table = np.zeros((4, 4))
    slope_table = np.zeros((4, 4))
    for column in range(4):
        others = [node_points[member] for member in range(4) if member != column]
        denominator = np.prod([node_points[column] - member for member in others])
        for quad_row in range(4):
            gauss_point = points[quad_row]
            value_table[quad_row, column] = (
                np.prod([gauss_point - member for member in others]) / denominator
            )
            slope_table[quad_row, column] = (
                sum(
                    (
                        np.prod(
                            [
                                gauss_point - others[position]
                                for position in range(3)
                                if position != skipped
                            ]
                        )
                        for skipped in range(3)
                    )
                )
                / denominator
            )
    centred = 2.0 * points - 1.0
    legendre_table = np.stack(
        [
            np.full(4, root_half),
            root_three_half * centred,
            root_five_half * 0.5 * (3.0 * centred**2 - 1.0),
        ],
        axis=1,
    )
    cube_table = (weights[:, None, None] * weights[None, :, None] * weights[None, None, :]).reshape(
        4, 4, 4, 1, 1, 1
    )
    return (value_table, slope_table, legendre_table, cube_table)


def as_table(operand):
    return jnp.asarray(np.asarray(operand), jnp.float32)


def contract(weights_table, operand, along):
    product = jnp.tensordot(
        as_table(weights_table), operand, axes=([1], [along]), precision=lax.Precision.HIGHEST
    )
    return jnp.moveaxis(product, 0, along)


def trace_along(modal_coefficients, vector, direction):
    return jnp.tensordot(
        as_table(vector),
        modal_coefficients,
        axes=([0], [direction]),
        precision=lax.Precision.HIGHEST,
    )


def spread_shape(vector, direction):
    broadcast_shape = [1] * 6
    broadcast_shape[direction] = 3
    return as_table(vector).reshape(broadcast_shape)


def boundary_terms(modal_coefficients, local_speed, right_ext, left_ext, speed_ext, direction):
    extent = modal_coefficients.shape[3 + direction]
    face_speed = 0.5 * (
        lax.slice_in_dim(speed_ext, 0, extent + 1, axis=direction)
        + lax.slice_in_dim(speed_ext, 1, extent + 2, axis=direction)
    )
    flux = (
        jnp.maximum(face_speed, 0.0)[None, None] * right_ext
        + jnp.minimum(face_speed, 0.0)[None, None] * left_ext
    )
    flux_left = lax.slice_in_dim(flux, 0, extent, axis=2 + direction)
    flux_right = lax.slice_in_dim(flux, 1, extent + 1, axis=2 + direction)
    lifted = contract(stiffness, modal_coefficients, direction)
    faces = spread_shape(plus_values, direction) * jnp.expand_dims(
        flux_right, direction
    ) - spread_shape(minus_values, direction) * jnp.expand_dims(flux_left, direction)
    return local_speed[None, None, None] * lifted - faces


def element_energy(corners, modal_coefficients):
    lagrange_values, lagrange_slopes, legendre_values, cube_weights = build_tables()
    along_value = contract(lagrange_values, corners, 1)
    along_slope = contract(lagrange_slopes, corners, 1)
    value_value = contract(lagrange_values, along_value, 2)
    jac_first = contract(lagrange_values, contract(lagrange_values, along_slope, 2), 3)
    jac_second = contract(lagrange_values, contract(lagrange_slopes, along_value, 2), 3)
    jac_third = contract(lagrange_slopes, value_value, 3)
    columns = (jac_first, jac_second, jac_third)
    sample = contract(
        legendre_values,
        contract(legendre_values, contract(legendre_values, modal_coefficients, 0), 1),
        2,
    )
    target_size = jnp.exp(theta_size * sample)
    inverse = 1.0 / target_size
    mapped = [
        [
            ((1.0 if component == column else 0.0) + columns[column][component]) * inverse
            for column in range(3)
        ]
        for component in range(3)
    ]
    metric = jnp.zeros_like(sample)
    for first_column in range(3):
        for second_column in range(3):
            gram_entry = (
                mapped[0][first_column] * mapped[0][second_column]
                + mapped[1][first_column] * mapped[1][second_column]
                + mapped[2][first_column] * mapped[2][second_column]
            )
            deviation = gram_entry - (1.0 if first_column == second_column else 0.0)
            metric = metric + deviation * deviation
    return jnp.sum(as_table(cube_weights) * target_size**3 * metric)


def element_corners(padded):
    gathered = padded
    for along, stack_axis in ((1, 1), (3, 2), (5, 3)):
        extent = (gathered.shape[along] - 1) // 3
        gathered = jnp.stack(
            [
                lax.slice_in_dim(
                    gathered, node_offset, node_offset + 3 * extent - 2, stride=3, axis=along
                )
                for node_offset in range(4)
            ],
            axis=stack_axis,
        )
    return gathered


def pad_one(operand, node_offset, along):
    config = [(0, 0, 0)] * operand.ndim
    config[along] = (node_offset, 3 - node_offset, 2)
    return lax.pad(operand, jnp.zeros((), operand.dtype), config)


def spread_corners(corner_grad):
    spread = corner_grad
    for stack_axis, along in ((3, 5), (2, 3), (1, 1)):
        pieces = [
            pad_one(
                lax.index_in_dim(spread, node_offset, axis=stack_axis, keepdims=False),
                node_offset,
                along,
            )
            for node_offset in range(4)
        ]
        spread = pieces[0] + pieces[1] + pieces[2] + pieces[3]
    return spread


def keep_rim(operand, direction, first_axis):
    for other_axis in range(3):
        if other_axis != direction:
            along = first_axis + other_axis
            operand = lax.slice_in_dim(operand, 1, operand.shape[along] - 1, axis=along)
    return operand


def trace_pair(modal_coefficients, direction):
    element_axis = 2 + direction
    extent = modal_coefficients.shape[3 + direction]
    right_trace = trace_along(modal_coefficients, plus_values, direction)
    left_trace = trace_along(modal_coefficients, minus_values, direction)
    last_right = lax.slice_in_dim(right_trace, extent - 1, extent, axis=element_axis)
    first_left = lax.slice_in_dim(left_trace, 0, 1, axis=element_axis)
    if direction == 0:
        from_low = passed_along(last_right, GX, 1)
        from_high = passed_along(first_left, GX, -1)
    elif direction == 1:
        from_low = passed_along(last_right, "gy", 1)
        from_high = passed_along(first_left, "gy", -1)
    else:
        from_low = passed_along(last_right, GZ, 1)
        from_high = passed_along(first_left, GZ, -1)
    right_ext = jnp.concatenate([from_low, right_trace], axis=element_axis)
    left_ext = jnp.concatenate([left_trace, from_high], axis=element_axis)
    return (right_ext, left_ext)


def upper_rim(nodal):
    received = passed_along(lax.slice_in_dim(nodal, 0, 1, axis=1), GX, -1)
    nodal = jnp.concatenate([nodal, received], axis=1)
    received = passed_along(lax.slice_in_dim(nodal, 0, 1, axis=2), "gy", -1)
    nodal = jnp.concatenate([nodal, received], axis=2)
    received = passed_along(lax.slice_in_dim(nodal, 0, 1, axis=3), GZ, -1)
    return jnp.concatenate([nodal, received], axis=3)


def on_device(displacement, size_field_modes, velocity):
    extent_x = size_field_modes.shape[1]
    extent_y = size_field_modes.shape[2]
    extent_z = size_field_modes.shape[3]
    modal_coefficients = size_field_modes.reshape(3, 3, 3, extent_x, extent_y, extent_z)
    fastest = one_axis_at_a_time(jnp.max(jnp.sum(jnp.abs(velocity), axis=0)), GX_GY_GZ)
    time_step = courant / jnp.maximum(fastest, 0.25)
    speed_rim = with_halo(velocity, ((GX, 1), ("gy", 2), (GZ, 3)), 1)
    speed_ext = [keep_rim(speed_rim[direction], direction, 0) for direction in range(3)]

    def advection_rate(current_field):
        pairs = [trace_pair(current_field, direction) for direction in range(3)]
        accumulated = jnp.zeros_like(current_field)
        for direction in range(3):
            accumulated = accumulated + boundary_terms(
                current_field,
                velocity[direction],
                pairs[direction][0],
                pairs[direction][1],
                speed_ext[direction],
                direction,
            )
        return 2.0 * accumulated

    for substep in range(SUBSTEPS):
        midway = modal_coefficients + time_step * advection_rate(modal_coefficients)
        modal_coefficients = 0.5 * modal_coefficients + 0.5 * (
            midway + time_step * advection_rate(midway)
        )
    widened_nodes = upper_rim(displacement)
    energy_local, corner_grad = jax.value_and_grad(element_energy)(
        element_corners(widened_nodes), modal_coefficients
    )
    elements = float(
        extent_x * extent_y * extent_z * lax.axis_size(GX) * lax.axis_size("gy") * lax.axis_size(GZ)
    )
    entries = 81.0 * elements
    energy_total = one_axis_at_a_time_2(energy_local, GX_GY_GZ)
    assembled = spread_corners(corner_grad)
    limit_x = assembled.shape[1] - 1
    received = passed_along(lax.slice_in_dim(assembled, limit_x, limit_x + 1, axis=1), GX, 1)
    assembled = jnp.concatenate(
        [
            lax.slice_in_dim(assembled, 0, 1, axis=1) + received,
            lax.slice_in_dim(assembled, 1, limit_x, axis=1),
        ],
        axis=1,
    )
    limit_y = assembled.shape[2] - 1
    received = passed_along(lax.slice_in_dim(assembled, limit_y, limit_y + 1, axis=2), "gy", 1)
    assembled = jnp.concatenate(
        [
            lax.slice_in_dim(assembled, 0, 1, axis=2) + received,
            lax.slice_in_dim(assembled, 1, limit_y, axis=2),
        ],
        axis=2,
    )
    limit_z = assembled.shape[3] - 1
    received = passed_along(lax.slice_in_dim(assembled, limit_z, limit_z + 1, axis=3), GZ, 1)
    gradient = jnp.concatenate(
        [
            lax.slice_in_dim(assembled, 0, 1, axis=3) + received,
            lax.slice_in_dim(assembled, 1, limit_z, axis=3),
        ],
        axis=3,
    )
    square_local = jnp.sum(gradient * gradient)
    square_total = one_axis_at_a_time_2(square_local, GX_GY_GZ)
    step_length = trial_step / jnp.sqrt(1.0 + square_total / entries)
    widened_trial = upper_rim(displacement - step_length * gradient)
    trial_local = element_energy(element_corners(widened_trial), modal_coefficients)
    trial_total = one_axis_at_a_time_2(trial_local, GX_GY_GZ)
    checks = jnp.stack([energy_total / elements, square_total / entries, trial_total / elements])
    return (modal_coefficients.reshape(27, extent_x, extent_y, extent_z), gradient, checks)


def solution(mesh):
    finer = Mesh(
        mesh.devices.reshape(4, 2, mesh.shape["gy"], 4, 2), ("gx_0", "gx_1", "gy", "gz_0", "gz_1")
    )
    return jax.shard_map(
        on_device,
        mesh=finer,
        in_specs=(P(None, GX, "gy", GZ), P(None, GX, "gy", GZ), P(None, GX, "gy", GZ)),
        out_specs=(P(None, GX, "gy", GZ), P(None, GX, "gy", GZ), P()),
        check_vma=False,
    )
```

profile of v0, /device:TPU:1, one launch (start us, length us, event | category | flops | bytes accessed | tf_op | source)
XLA Modules:
  0.0 456.1 jit_solution(2346756452224678851)
XLA Ops:
  8.1 5.8 %collective-permute-start = (f32[3,2,2,1]{3,2,1,0:T(2,128)S(1)}, f32[3,2,2,1]{3,2,1,0:T(2,128)S(1)}, u32[]{:S(2)}, u32[]{:S(2)}) collective-permute-start(f32[3,2,2,1]{3,2,1,0:T(2,128)S(1)} %get-tuple-element.128), channel_id=1, source_target_pairs={{0,1},{1,2},{2,3},{3,4},{4,5},{5,6},{6,7},{7,0},{8,9},{9,10},{10,1... | collective-permute-start | bytes 152 | tf_op jit(solution)/shard_map/ppermute | solution.py:44
  17.6 9.8 %pmax.35 = f32[]{:T(128)} all-reduce(f32[]{:T(128)} %reduce_max.9), channel_id=1, replica_groups=mesh['gx_0'=4,'gx_1'=2,'gy'=4,'gz_0'=4,'gz_1'=2] {'gx_0'}, use_global_device_ids=true, to_apply=%region_2.0 | all-reduce | flops 1 | bytes 8 | tf_op jit(solution)/shard_map/pmax | solution.py:32
  27.6 5.3 %pmax.36 = f32[]{:T(128)} all-reduce(f32[]{:T(128)} %pmax.35), channel_id=1, replica_groups=mesh['gx_0'=4,'gx_1'=2,'gy'=4,'gz_0'=4,'gz_1'=2] {'gx_1'}, use_global_device_ids=true, to_apply=%region_3.0 | all-reduce | flops 1 | bytes 8 | tf_op jit(solution)/shard_map/pmax | solution.py:32
  33.2 7.9 %pmax.37 = f32[]{:T(128)} all-reduce(f32[]{:T(128)} %pmax.36), channel_id=1, replica_groups=mesh['gx_0'=4,'gx_1'=2,'gy'=4,'gz_0'=4,'gz_1'=2] {'gy'}, use_global_device_ids=true, to_apply=%region_4.0 | all-reduce | flops 1 | bytes 8 | tf_op jit(solution)/shard_map/pmax | solution.py:32
  41.1 9.3 %pmax.38 = f32[]{:T(128)} all-reduce(f32[]{:T(128)} %pmax.37), channel_id=1, replica_groups=mesh['gx_0'=4,'gx_1'=2,'gy'=4,'gz_0'=4,'gz_1'=2] {'gz_0'}, use_global_device_ids=true, to_apply=%region_5.0 | all-reduce | flops 1 | bytes 8 | tf_op jit(solution)/shard_map/pmax | solution.py:32
  50.5 8.3 %pmax.39 = f32[]{:T(128)} all-reduce(f32[]{:T(128)} %pmax.38), channel_id=1, replica_groups=mesh['gx_0'=4,'gx_1'=2,'gy'=4,'gz_0'=4,'gz_1'=2] {'gz_1'}, use_global_device_ids=true, to_apply=%region_6.0 | all-reduce | flops 1 | bytes 8 | tf_op jit(solution)/shard_map/pmax | solution.py:32
  60.6 5.5 %collective-permute-done.5 = f32[3,2,2,1]{3,2,1,0:T(2,128)S(1)} collective-permute-done((f32[3,2,2,1]{3,2,1,0:T(2,128)S(1)}, f32[3,2,2,1]{3,2,1,0:T(2,128)S(1)}, u32[]{:S(2)}, u32[]{:S(2)}) %collective-permute-start.5) | collective-permute-done | bytes 80 | tf_op jit(solution)/shard_map/ppermute | solution.py:45
  66.2 6.7 %collective-permute-start.7 = (f32[3,3,1,2,128]{4,3,2,1,0:T(2,128)S(1)}, f32[3,3,1,2,128]{4,3,2,1,0:T(2,128)S(1)}, u32[]{:S(2)}, u32[]{:S(2)}) collective-permute-start(f32[3,3,1,2,128]{4,3,2,1,0:T(2,128)S(1)} %slice.822), channel_id=1, source_target_pairs={{0,224},{32,0},{64,32},{96,64},{128,96},{160,128},{192,160},{224,1... | collective-permute-start | bytes 27656 | tf_op jit(solution)/shard_map/ppermute | solution.py:27
  75.3 6.7 %collective-permute-start.11 = (f32[3,3,2,2,1]{4,0,3,2,1:T(4,128)S(1)}, f32[3,3,2,2,1]{4,0,3,2,1:T(4,128)S(1)}, u32[]{:S(2)}, u32[]{:S(2)}) collective-permute-start(f32[3,3,2,2,1]{4,0,3,2,1:T(4,128)S(1)} %bitcast.1062), channel_id=1, source_target_pairs={{0,7},{1,0},{2,1},{3,2},{4,3},{5,4},{6,5},{7,6},{8,15},{9,8},{10,9... | collective-permute-start | bytes 440 | tf_op jit(solution)/shard_map/ppermute | solution.py:27
  94.4 7.5 %collective-permute-start.17 = (f32[3,3,2,2,1]{4,0,3,2,1:T(4,128)S(1)}, f32[3,3,2,2,1]{4,0,3,2,1:T(4,128)S(1)}, u32[]{:S(2)}, u32[]{:S(2)}) collective-permute-start(f32[3,3,2,2,1]{4,0,3,2,1:T(4,128)S(1)} %bitcast.1068), channel_id=1, source_target_pairs={{0,7},{1,0},{2,1},{3,2},{4,3},{5,4},{6,5},{7,6},{8,15},{9,8},{10,9... | collective-permute-start | bytes 440 | tf_op jit(solution)/shard_map/ppermute | solution.py:27
  114.5 5.9 %collective-permute-start.23 = (f32[3,3,2,2,1]{4,0,3,2,1:T(4,128)S(1)}, f32[3,3,2,2,1]{4,0,3,2,1:T(4,128)S(1)}, u32[]{:S(2)}, u32[]{:S(2)}) collective-permute-start(f32[3,3,2,2,1]{4,0,3,2,1:T(4,128)S(1)} %bitcast.1074), channel_id=1, source_target_pairs={{0,7},{1,0},{2,1},{3,2},{4,3},{5,4},{6,5},{7,6},{8,15},{9,8},{10,9... | collective-permute-start | bytes 440 | tf_op jit(solution)/shard_map/ppermute | solution.py:27
  121.5 8.7 %collective-permute-start.21 = (f32[3,3,2,1,128]{4,0,3,2,1:T(4,128)S(1)}, f32[3,3,2,1,128]{4,0,3,2,1:T(4,128)S(1)}, u32[]{:S(2)}, u32[]{:S(2)}) collective-permute-start(f32[3,3,2,1,128]{4,0,3,2,1:T(4,128)S(1)} %slice.856), channel_id=1, source_target_pairs={{0,24},{8,0},{16,8},{24,16},{1,25},{9,1},{17,9},{25,17},{2,26},{10... | collective-permute-start | bytes 27656 | tf_op jit(solution)/shard_map/ppermute | solution.py:27
  139.8 7.5 %collective-permute-start.29 = (f32[3,3,2,2,1]{4,0,3,2,1:T(4,128)S(1)}, f32[3,3,2,2,1]{4,0,3,2,1:T(4,128)S(1)}, u32[]{:S(2)}, u32[]{:S(2)}) collective-permute-start(f32[3,3,2,2,1]{4,0,3,2,1:T(4,128)S(1)} %bitcast.1064), channel_id=1, source_target_pairs={{0,7},{1,0},{2,1},{3,2},{4,3},{5,4},{6,5},{7,6},{8,15},{9,8},{10,9... | collective-permute-start | bytes 440 | tf_op jit(solution)/shard_map/ppermute | solution.py:27
  158.7 7.5 %collective-permute-start.35 = (f32[3,3,2,2,1]{4,0,3,2,1:T(4,128)S(1)}, f32[3,3,2,2,1]{4,0,3,2,1:T(4,128)S(1)}, u32[]{:S(2)}, u32[]{:S(2)}) collective-permute-start(f32[3,3,2,2,1]{4,0,3,2,1:T(4,128)S(1)} %bitcast.1070), channel_id=1, source_target_pairs={{0,7},{1,0},{2,1},{3,2},{4,3},{5,4},{6,5},{7,6},{8,15},{9,8},{10,9... | collective-permute-start | bytes 440 | tf_op jit(solution)/shard_map/ppermute | solution.py:27
  177.9 6.8 %collective-permute-start.41 = (f32[3,3,2,2,1]{4,0,3,2,1:T(4,128)S(1)}, f32[3,3,2,2,1]{4,0,3,2,1:T(4,128)S(1)}, u32[]{:S(2)}, u32[]{:S(2)}) collective-permute-start(f32[3,3,2,2,1]{4,0,3,2,1:T(4,128)S(1)} %bitcast.1072), channel_id=1, source_target_pairs={{0,7},{1,0},{2,1},{3,2},{4,3},{5,4},{6,5},{7,6},{8,15},{9,8},{10,9... | collective-permute-start | bytes 440 | tf_op jit(solution)/shard_map/ppermute | solution.py:27
  192.2 3.5 collective-permute-start.43
  197.8 5.8 %collective-permute-start.47 = (f32[3,3,2,2,1]{4,0,3,2,1:T(4,128)S(1)}, f32[3,3,2,2,1]{4,0,3,2,1:T(4,128)S(1)}, u32[]{:S(2)}, u32[]{:S(2)}) collective-permute-start(f32[3,3,2,2,1]{4,0,3,2,1:T(4,128)S(1)} %bitcast.1076), channel_id=1, source_target_pairs={{0,7},{1,0},{2,1},{3,2},{4,3},{5,4},{6,5},{7,6},{8,15},{9,8},{10,9... | collective-permute-start | bytes 440 | tf_op jit(solution)/shard_map/ppermute | solution.py:27
  206.4 6.3 %collective-permute-start.56 = (f32[3,7,7,1]{3,2,1,0:T(8,128)S(1)}, f32[3,7,7,1]{3,2,1,0:T(8,128)S(1)}, u32[]{:S(2)}, u32[]{:S(2)}) collective-permute-start(f32[3,7,7,1]{3,2,1,0:T(8,128)S(1)} %pad_maximum_fusion.11), channel_id=1, source_target_pairs={{0,7},{1,0},{2,1},{3,2},{4,3},{5,4},{6,5},{7,6},{8,15},{9,8},{10,9... | collective-permute-start | bytes 1772 | tf_op jit(solution)/shard_map/ppermute | solution.py:27
  215.8 3.9 slice.763
  219.7 3.9 slice.762
  223.5 3.9 slice.761
  227.4 3.9 slice.760
  242.0 3.0 collective-permute-start.49
  247.6 4.0 collective-permute-start.52
  251.6 4.2 collective-permute-start.53
  272.5 8.1 %pad.91 = f32[3,4,4,2,2,385]{5,1,4,3,2,0:T(4,128)S(1)} pad(f32[3,4,4,2,2,128]{5,1,4,3,2,0:T(4,128)S(1)} %get-tuple-element.47, f32[]{:T(128)} %constant.19.clone.1), padding=0_0_0x0_0_0x0_0_0x0_0_0x0_0_0x1_2_2 | pad | bytes 393988 | tf_op jit(solution)/shard_map/pad | solution.py:212
  280.6 7.8 %pad.90 = f32[3,4,4,2,2,385]{5,1,4,3,2,0:T(4,128)S(1)} pad(f32[3,4,4,2,2,128]{5,1,4,3,2,0:T(4,128)S(1)} %get-tuple-element.48, f32[]{:T(128)} %constant.19.clone.1), padding=0_0_0x0_0_0x0_0_0x0_0_0x0_0_0x0_3_2 | pad | bytes 393988 | tf_op jit(solution)/shard_map/pad | solution.py:212
  288.4 7.7 %pad.93 = f32[3,4,4,2,2,385]{5,1,4,3,2,0:T(4,128)S(1)} pad(f32[3,4,4,2,2,128]{5,1,4,3,2,0:T(4,128)S(1)} %get-tuple-element.49, f32[]{:T(128)} %constant.19.clone.1), padding=0_0_0x0_0_0x0_0_0x0_0_0x0_0_0x3_0_2 | pad | bytes 393988 | tf_op jit(solution)/shard_map/pad | solution.py:212
  296.2 7.8 %pad.92 = f32[3,4,4,2,2,385]{5,1,4,3,2,0:T(4,128)S(1)} pad(f32[3,4,4,2,2,128]{5,1,4,3,2,0:T(4,128)S(1)} %get-tuple-element.50, f32[]{:T(128)} %constant.19.clone.1), padding=0_0_0x0_0_0x0_0_0x0_0_0x0_0_0x2_1_2 | pad | bytes 393988 | tf_op jit(solution)/shard_map/pad | solution.py:212
  310.6 4.1 collective-permute-done.58
  317.9 6.3 %collective-permute-done.59 = f32[3,6,6,1]{3,1,2,0:T(8,128)S(1)} collective-permute-done((f32[3,6,6,1]{3,1,2,0:T(8,128)S(1)}, f32[3,6,6,1]{3,1,2,0:T(8,128)S(1)}, u32[]{:S(2)}, u32[]{:S(2)}) %collective-permute-start.59) | collective-permute-done | bytes 464 | tf_op jit(solution)/shard_map/ppermute | solution.py:27
  324.9 11.6 %psum.110 = f32[]{:T(128)} all-reduce(f32[]{:T(128)} %get-tuple-element.21), channel_id=1, replica_groups=mesh['gx_0'=4,'gx_1'=2,'gy'=4,'gz_0'=4,'gz_1'=2] {'gx_0'}, use_global_device_ids=true, to_apply=%region_14.15 | all-reduce | flops 1 | bytes 8 | tf_op jit(solution)/shard_map/psum | solution.py:58
  336.5 6.9 %psum.111 = f32[]{:T(128)} all-reduce(f32[]{:T(128)} %psum.110), channel_id=1, replica_groups=mesh['gx_0'=4,'gx_1'=2,'gy'=4,'gz_0'=4,'gz_1'=2] {'gx_1'}, use_global_device_ids=true, to_apply=%region_15.16 | all-reduce | flops 1 | bytes 8 | tf_op jit(solution)/shard_map/psum | solution.py:58
  343.4 6.7 %psum.112 = f32[]{:T(128)} all-reduce(f32[]{:T(128)} %psum.111), channel_id=1, replica_groups=mesh['gx_0'=4,'gx_1'=2,'gy'=4,'gz_0'=4,'gz_1'=2] {'gy'}, use_global_device_ids=true, to_apply=%region_16.17 | all-reduce | flops 1 | bytes 8 | tf_op jit(solution)/shard_map/psum | solution.py:58
  350.1 9.3 %psum.113 = f32[]{:T(128)} all-reduce(f32[]{:T(128)} %psum.112), channel_id=1, replica_groups=mesh['gx_0'=4,'gx_1'=2,'gy'=4,'gz_0'=4,'gz_1'=2] {'gz_0'}, use_global_device_ids=true, to_apply=%region_17.18 | all-reduce | flops 1 | bytes 8 | tf_op jit(solution)/shard_map/psum | solution.py:58
  359.4 8.3 %psum.114 = f32[]{:T(128)} all-reduce(f32[]{:T(128)} %psum.113), channel_id=1, replica_groups=mesh['gx_0'=4,'gx_1'=2,'gy'=4,'gz_0'=4,'gz_1'=2] {'gz_1'}, use_global_device_ids=true, to_apply=%region_18.19 | all-reduce | flops 1 | bytes 8 | tf_op jit(solution)/shard_map/psum | solution.py:58
  368.5 5.2 %collective-permute-start.60 = (f32[3,1,6,384]{3,1,2,0:T(1,128)S(1)}, f32[3,1,6,384]{3,1,2,0:T(1,128)S(1)}, u32[]{:S(2)}, u32[]{:S(2)}) collective-permute-start(f32[3,1,6,384]{3,1,2,0:T(1,128)S(1)} %slice.951), channel_id=1, source_target_pairs={{0,224},{32,0},{64,32},{96,64},{128,96},{160,128},{192,160},{224,1... | collective-permute-start | bytes 82952 | tf_op jit(solution)/shard_map/ppermute | solution.py:27
  373.7 3.1 collective-permute-done.60
  383.1 6.3 %collective-permute-done.62 = f32[3,7,7,1]{3,1,2,0:T(8,128)S(1)} collective-permute-done((f32[3,7,7,1]{3,1,2,0:T(8,128)S(1)}, f32[3,7,7,1]{3,1,2,0:T(8,128)S(1)}, u32[]{:S(2)}, u32[]{:S(2)}) %collective-permute-start.62) | collective-permute-done | bytes 620 | tf_op jit(solution)/shard_map/ppermute | solution.py:27
  391.4 3.9 slice.808
  395.3 3.9 slice.807
  399.1 3.9 slice.806
  403.0 3.9 slice.805
  415.5 8.2 %all-reduce.27 = (f32[]{:T(128)}, f32[]{:T(128)}) all-reduce(f32[]{:T(128)} %get-tuple-element.10, f32[]{:T(128)} %get-tuple-element.9), channel_id=1, replica_groups=mesh['gx_0'=4,'gx_1'=2,'gy'=4,'gz_0'=4,'gz_1'=2] {'gx_0'}, use_global_device_ids=true, to_apply=%region_20.21 | all-reduce | flops 2 | bytes 16 | tf_op jit(solution)/shard_map/psum | solution.py:58
  423.7 5.8 %all-reduce.29 = (f32[]{:T(128)}, f32[]{:T(128)}) all-reduce(f32[]{:T(128)} %get-tuple-element.15, f32[]{:T(128)} %get-tuple-element.16), channel_id=1, replica_groups=mesh['gx_0'=4,'gx_1'=2,'gy'=4,'gz_0'=4,'gz_1'=2] {'gx_1'}, use_global_device_ids=true, to_apply=%region_21.22 | all-reduce | flops 2 | bytes 16 | tf_op jit(solution)/shard_map/psum | solution.py:58
  429.5 9.5 %all-reduce.26 = (f32[]{:T(128)}, f32[]{:T(128)}) all-reduce(f32[]{:T(128)} %get-tuple-element.19, f32[]{:T(128)} %get-tuple-element.20), channel_id=1, replica_groups=mesh['gx_0'=4,'gx_1'=2,'gy'=4,'gz_0'=4,'gz_1'=2] {'gy'}, use_global_device_ids=true, to_apply=%region_22.23 | all-reduce | flops 2 | bytes 16 | tf_op jit(solution)/shard_map/psum | solution.py:58
  439.0 6.6 %all-reduce.25 = (f32[]{:T(128)}, f32[]{:T(128)}) all-reduce(f32[]{:T(128)} %get-tuple-element.13, f32[]{:T(128)} %get-tuple-element.14), channel_id=1, replica_groups=mesh['gx_0'=4,'gx_1'=2,'gy'=4,'gz_0'=4,'gz_1'=2] {'gz_0'}, use_global_device_ids=true, to_apply=%region_23.24 | all-reduce | flops 2 | bytes 16 | tf_op jit(solution)/shard_map/psum | solution.py:58
  445.6 8.4 %all-reduce.28 = (f32[]{:T(128)}, f32[]{:T(128)}) all-reduce(f32[]{:T(128)} %get-tuple-element.11, f32[]{:T(128)} %get-tuple-element.12), channel_id=1, replica_groups=mesh['gx_0'=4,'gx_1'=2,'gy'=4,'gz_0'=4,'gz_1'=2] {'gz_1'}, use_global_device_ids=true, to_apply=%region_24.25 | all-reduce | flops 2 | bytes 16 | tf_op jit(solution)/shard_map/psum | solution.py:58
  (424 shorter events, 145.4 us)
Async XLA Ops:
  1.4 71.4 %collective-permute-start.1 = (f32[3,2,1,128]{3,2,1,0:T(1,128)S(1)}, f32[3,2,1,128]{3,2,1,0:T(1,128)S(1)}, u32[]{:S(2)}, u32[]{:S(2)}) collective-permute-start(f32[3,2,1,128]{3,2,1,0:T(1,128)S(1)} %get-tuple-element.130), channel_id=1, source_target_pairs={{0,8},{8,16},{16,24},{24,0},{1,9},{9,17},{17,25},{25,1},{2,10},{10... | collective-permute-start | bytes 9224 | tf_op jit(solution)/shard_map/ppermute | solution.py:44
  3.5 70.8 %collective-permute-start.4 = (f32[3,2,1,128]{3,2,1,0:T(1,128)S(1)}, f32[3,2,1,128]{3,2,1,0:T(1,128)S(1)}, u32[]{:S(2)}, u32[]{:S(2)}) collective-permute-start(f32[3,2,1,128]{3,2,1,0:T(1,128)S(1)} %get-tuple-element.131), channel_id=1, source_target_pairs={{8,0},{16,8},{24,16},{0,24},{9,1},{17,9},{25,17},{1,25},{10,2},{18... | collective-permute-start | bytes 9224 | tf_op jit(solution)/shard_map/ppermute | solution.py:45
  4.9 69.6 %collective-permute-start.2 = (f32[3,1,2,128]{3,2,1,0:T(2,128)S(1)}, f32[3,1,2,128]{3,2,1,0:T(2,128)S(1)}, u32[]{:S(2)}, u32[]{:S(2)}) collective-permute-start(f32[3,1,2,128]{3,2,1,0:T(2,128)S(1)} %get-tuple-element.126), channel_id=1, source_target_pairs={{0,32},{32,64},{64,96},{96,128},{128,160},{160,192},{192,224},{224... | collective-permute-start | bytes 9224 | tf_op jit(solution)/shard_map/ppermute | solution.py:44
  7.8 67.5 %collective-permute-start.3 = (f32[3,1,2,128]{3,2,1,0:T(2,128)S(1)}, f32[3,1,2,128]{3,2,1,0:T(2,128)S(1)}, u32[]{:S(2)}, u32[]{:S(2)}) collective-permute-start(f32[3,1,2,128]{3,2,1,0:T(2,128)S(1)} %get-tuple-element.127), channel_id=1, source_target_pairs={{32,0},{64,32},{96,64},{128,96},{160,128},{192,160},{224,192},{0,2... | collective-permute-start | bytes 9224 | tf_op jit(solution)/shard_map/ppermute | solution.py:45
  8.1 51.6 %collective-permute-start = (f32[3,2,2,1]{3,2,1,0:T(2,128)S(1)}, f32[3,2,2,1]{3,2,1,0:T(2,128)S(1)}, u32[]{:S(2)}, u32[]{:S(2)}) collective-permute-start(f32[3,2,2,1]{3,2,1,0:T(2,128)S(1)} %get-tuple-element.128), channel_id=1, source_target_pairs={{0,1},{1,2},{2,3},{3,4},{4,5},{5,6},{6,7},{7,0},{8,9},{9,10},{10,1... | collective-permute-start | bytes 152 | tf_op jit(solution)/shard_map/ppermute | solution.py:44
  66.2 19.6 %collective-permute-start.7 = (f32[3,3,1,2,128]{4,3,2,1,0:T(2,128)S(1)}, f32[3,3,1,2,128]{4,3,2,1,0:T(2,128)S(1)}, u32[]{:S(2)}, u32[]{:S(2)}) collective-permute-start(f32[3,3,1,2,128]{4,3,2,1,0:T(2,128)S(1)} %slice.822), channel_id=1, source_target_pairs={{0,224},{32,0},{64,32},{96,64},{128,96},{160,128},{192,160},{224,1... | collective-permute-start | bytes 27656 | tf_op jit(solution)/shard_map/ppermute | solution.py:27
  72.8 12.9 %collective-permute-start.6 = (f32[3,3,1,2,128]{4,3,2,1,0:T(2,128)S(1)}, f32[3,3,1,2,128]{4,3,2,1,0:T(2,128)S(1)}, u32[]{:S(2)}, u32[]{:S(2)}) collective-permute-start(f32[3,3,1,2,128]{4,3,2,1,0:T(2,128)S(1)} %slice.821), channel_id=1, source_target_pairs={{0,32},{32,64},{64,96},{96,128},{128,160},{160,192},{192,224},{224... | collective-permute-start | bytes 27656 | tf_op jit(solution)/shard_map/ppermute | solution.py:27
  74.3 11.5 %collective-permute-start.9 = (f32[3,3,2,1,128]{4,0,3,2,1:T(4,128)S(1)}, f32[3,3,2,1,128]{4,0,3,2,1:T(4,128)S(1)}, u32[]{:S(2)}, u32[]{:S(2)}) collective-permute-start(f32[3,3,2,1,128]{4,0,3,2,1:T(4,128)S(1)} %slice.829), channel_id=1, source_target_pairs={{0,24},{8,0},{16,8},{24,16},{1,25},{9,1},{17,9},{25,17},{2,26},{10... | collective-permute-start | bytes 27656 | tf_op jit(solution)/shard_map/ppermute | solution.py:27
  74.5 8.8 %collective-permute-start.10 = (f32[3,3,2,2,1]{4,0,3,2,1:T(4,128)S(1)}, f32[3,3,2,2,1]{4,0,3,2,1:T(4,128)S(1)}, u32[]{:S(2)}, u32[]{:S(2)}) collective-permute-start(f32[3,3,2,2,1]{4,0,3,2,1:T(4,128)S(1)} %slice.835), channel_id=1, source_target_pairs={{0,1},{1,2},{2,3},{3,4},{4,5},{5,6},{6,7},{7,0},{8,9},{9,10},{10,1... | collective-permute-start | bytes 440 | tf_op jit(solution)/shard_map/ppermute | solution.py:27
  75.3 9.3 %collective-permute-start.11 = (f32[3,3,2,2,1]{4,0,3,2,1:T(4,128)S(1)}, f32[3,3,2,2,1]{4,0,3,2,1:T(4,128)S(1)}, u32[]{:S(2)}, u32[]{:S(2)}) collective-permute-start(f32[3,3,2,2,1]{4,0,3,2,1:T(4,128)S(1)} %bitcast.1062), channel_id=1, source_target_pairs={{0,7},{1,0},{2,1},{3,2},{4,3},{5,4},{6,5},{7,6},{8,15},{9,8},{10,9... | collective-permute-start | bytes 440 | tf_op jit(solution)/shard_map/ppermute | solution.py:27
  84.6 55.2 %collective-permute-start.54 = (f32[3,1,6,384]{3,2,1,0:T(8,128)S(1)}, f32[3,1,6,384]{3,2,1,0:T(8,128)S(1)}, u32[]{:S(2)}, u32[]{:S(2)}) collective-permute-start(f32[3,1,6,384]{3,2,1,0:T(8,128)S(1)} %slice.749), channel_id=1, source_target_pairs={{0,224},{32,0},{64,32},{96,64},{128,96},{160,128},{192,160},{224,1... | collective-permute-start | bytes 82952 | tf_op jit(solution)/shard_map/ppermute | solution.py:27
  90.4 14.4 %collective-permute-start.13 = (f32[3,3,1,2,128]{4,3,2,1,0:T(2,128)S(1)}, f32[3,3,1,2,128]{4,3,2,1,0:T(2,128)S(1)}, u32[]{:S(2)}, u32[]{:S(2)}) collective-permute-start(f32[3,3,1,2,128]{4,3,2,1,0:T(2,128)S(1)} %slice.840), channel_id=1, source_target_pairs={{0,224},{32,0},{64,32},{96,64},{128,96},{160,128},{192,160},{224,1... | collective-permute-start | bytes 27656 | tf_op jit(solution)/shard_map/ppermute | solution.py:27
  92.0 12.8 %collective-permute-start.12 = (f32[3,3,1,2,128]{4,3,2,1,0:T(2,128)S(1)}, f32[3,3,1,2,128]{4,3,2,1,0:T(2,128)S(1)}, u32[]{:S(2)}, u32[]{:S(2)}) collective-permute-start(f32[3,3,1,2,128]{4,3,2,1,0:T(2,128)S(1)} %slice.839), channel_id=1, source_target_pairs={{0,32},{32,64},{64,96},{96,128},{128,160},{160,192},{192,224},{224... | collective-permute-start | bytes 27656 | tf_op jit(solution)/shard_map/ppermute | solution.py:27
  94.4 8.7 %collective-permute-start.16 = (f32[3,3,2,2,1]{4,0,3,2,1:T(4,128)S(1)}, f32[3,3,2,2,1]{4,0,3,2,1:T(4,128)S(1)}, u32[]{:S(2)}, u32[]{:S(2)}) collective-permute-start(f32[3,3,2,2,1]{4,0,3,2,1:T(4,128)S(1)} %slice.847), channel_id=1, source_target_pairs={{0,1},{1,2},{2,3},{3,4},{4,5},{5,6},{6,7},{7,0},{8,9},{9,10},{10,1... | collective-permute-start | bytes 440 | tf_op jit(solution)/shard_map/ppermute | solution.py:27
  94.4 8.7 %collective-permute-start.17 = (f32[3,3,2,2,1]{4,0,3,2,1:T(4,128)S(1)}, f32[3,3,2,2,1]{4,0,3,2,1:T(4,128)S(1)}, u32[]{:S(2)}, u32[]{:S(2)}) collective-permute-start(f32[3,3,2,2,1]{4,0,3,2,1:T(4,128)S(1)} %bitcast.1068), channel_id=1, source_target_pairs={{0,7},{1,0},{2,1},{3,2},{4,3},{5,4},{6,5},{7,6},{8,15},{9,8},{10,9... | collective-permute-start | bytes 440 | tf_op jit(solution)/shard_map/ppermute | solution.py:27
  109.5 22.4 %collective-permute-start.19 = (f32[3,3,1,2,128]{4,3,2,1,0:T(2,128)S(1)}, f32[3,3,1,2,128]{4,3,2,1,0:T(2,128)S(1)}, u32[]{:S(2)}, u32[]{:S(2)}) collective-permute-start(f32[3,3,1,2,128]{4,3,2,1,0:T(2,128)S(1)} %slice.852), channel_id=1, source_target_pairs={{0,224},{32,0},{64,32},{96,64},{128,96},{160,128},{192,160},{224,1... | collective-permute-start | bytes 27656 | tf_op jit(solution)/shard_map/ppermute | solution.py:27
  110.6 21.2 %collective-permute-start.18 = (f32[3,3,1,2,128]{4,3,2,1,0:T(2,128)S(1)}, f32[3,3,1,2,128]{4,3,2,1,0:T(2,128)S(1)}, u32[]{:S(2)}, u32[]{:S(2)}) collective-permute-start(f32[3,3,1,2,128]{4,3,2,1,0:T(2,128)S(1)} %slice.851), channel_id=1, source_target_pairs={{0,32},{32,64},{64,96},{96,128},{128,160},{160,192},{192,224},{224... | collective-permute-start | bytes 27656 | tf_op jit(solution)/shard_map/ppermute | solution.py:27
  112.6 8.9 %collective-permute-start.22 = (f32[3,3,2,2,1]{4,0,3,2,1:T(4,128)S(1)}, f32[3,3,2,2,1]{4,0,3,2,1:T(4,128)S(1)}, u32[]{:S(2)}, u32[]{:S(2)}) collective-permute-start(f32[3,3,2,2,1]{4,0,3,2,1:T(4,128)S(1)} %slice.859), channel_id=1, source_target_pairs={{0,1},{1,2},{2,3},{3,4},{4,5},{5,6},{6,7},{7,0},{8,9},{9,10},{10,1... | collective-permute-start | bytes 440 | tf_op jit(solution)/shard_map/ppermute | solution.py:27
  114.5 15.8 %collective-permute-start.23 = (f32[3,3,2,2,1]{4,0,3,2,1:T(4,128)S(1)}, f32[3,3,2,2,1]{4,0,3,2,1:T(4,128)S(1)}, u32[]{:S(2)}, u32[]{:S(2)}) collective-permute-start(f32[3,3,2,2,1]{4,0,3,2,1:T(4,128)S(1)} %bitcast.1074), channel_id=1, source_target_pairs={{0,7},{1,0},{2,1},{3,2},{4,3},{5,4},{6,5},{7,6},{8,15},{9,8},{10,9... | collective-permute-start | bytes 440 | tf_op jit(solution)/shard_map/ppermute | solution.py:27
  121.5 11.3 %collective-permute-start.21 = (f32[3,3,2,1,128]{4,0,3,2,1:T(4,128)S(1)}, f32[3,3,2,1,128]{4,0,3,2,1:T(4,128)S(1)}, u32[]{:S(2)}, u32[]{:S(2)}) collective-permute-start(f32[3,3,2,1,128]{4,0,3,2,1:T(4,128)S(1)} %slice.856), channel_id=1, source_target_pairs={{0,24},{8,0},{16,8},{24,16},{1,25},{9,1},{17,9},{25,17},{2,26},{10... | collective-permute-start | bytes 27656 | tf_op jit(solution)/shard_map/ppermute | solution.py:27
  136.7 14.6 %collective-permute-start.25 = (f32[3,3,1,2,128]{4,3,2,1,0:T(2,128)S(1)}, f32[3,3,1,2,128]{4,3,2,1,0:T(2,128)S(1)}, u32[]{:S(2)}, u32[]{:S(2)}) collective-permute-start(f32[3,3,1,2,128]{4,3,2,1,0:T(2,128)S(1)} %slice.864), channel_id=1, source_target_pairs={{0,224},{32,0},{64,32},{96,64},{128,96},{160,128},{192,160},{224,1... | collective-permute-start | bytes 27656 | tf_op jit(solution)/shard_map/ppermute | solution.py:27
  138.3 13.1 %collective-permute-start.24 = (f32[3,3,1,2,128]{4,3,2,1,0:T(2,128)S(1)}, f32[3,3,1,2,128]{4,3,2,1,0:T(2,128)S(1)}, u32[]{:S(2)}, u32[]{:S(2)}) collective-permute-start(f32[3,3,1,2,128]{4,3,2,1,0:T(2,128)S(1)} %slice.863), channel_id=1, source_target_pairs={{0,32},{32,64},{64,96},{96,128},{128,160},{160,192},{192,224},{224... | collective-permute-start | bytes 27656 | tf_op jit(solution)/shard_map/ppermute | solution.py:27
  139.5 11.9 %collective-permute-start.27 = (f32[3,3,2,1,128]{4,0,3,2,1:T(4,128)S(1)}, f32[3,3,2,1,128]{4,0,3,2,1:T(4,128)S(1)}, u32[]{:S(2)}, u32[]{:S(2)}) collective-permute-start(f32[3,3,2,1,128]{4,0,3,2,1:T(4,128)S(1)} %slice.868), channel_id=1, source_target_pairs={{0,24},{8,0},{16,8},{24,16},{1,25},{9,1},{17,9},{25,17},{2,26},{10... | collective-permute-start | bytes 27656 | tf_op jit(solution)/shard_map/ppermute | solution.py:27
  139.8 8.7 %collective-permute-start.28 = (f32[3,3,2,2,1]{4,0,3,2,1:T(4,128)S(1)}, f32[3,3,2,2,1]{4,0,3,2,1:T(4,128)S(1)}, u32[]{:S(2)}, u32[]{:S(2)}) collective-permute-start(f32[3,3,2,2,1]{4,0,3,2,1:T(4,128)S(1)} %slice.871), channel_id=1, source_target_pairs={{0,1},{1,2},{2,3},{3,4},{4,5},{5,6},{6,7},{7,0},{8,9},{9,10},{10,1... | collective-permute-start | bytes 440 | tf_op jit(solution)/shard_map/ppermute | solution.py:27
  139.8 10.0 %collective-permute-start.29 = (f32[3,3,2,2,1]{4,0,3,2,1:T(4,128)S(1)}, f32[3,3,2,2,1]{4,0,3,2,1:T(4,128)S(1)}, u32[]{:S(2)}, u32[]{:S(2)}) collective-permute-start(f32[3,3,2,2,1]{4,0,3,2,1:T(4,128)S(1)} %bitcast.1064), channel_id=1, source_target_pairs={{0,7},{1,0},{2,1},{3,2},{4,3},{5,4},{6,5},{7,6},{8,15},{9,8},{10,9... | collective-permute-start | bytes 440 | tf_op jit(solution)/shard_map/ppermute | solution.py:27
  149.8 56.5 %collective-permute-start.55 = (f32[3,7,1,384]{3,2,1,0:T(1,128)S(1)}, f32[3,7,1,384]{3,2,1,0:T(1,128)S(1)}, u32[]{:S(2)}, u32[]{:S(2)}) collective-permute-start(f32[3,7,1,384]{3,2,1,0:T(1,128)S(1)} %slice.923), channel_id=1, source_target_pairs={{0,24},{8,0},{16,8},{24,16},{1,25},{9,1},{17,9},{25,17},{2,26},{10... | collective-permute-start | bytes 96776 | tf_op jit(solution)/shard_map/ppermute | solution.py:27
  154.9 14.4 %collective-permute-start.31 = (f32[3,3,1,2,128]{4,3,2,1,0:T(2,128)S(1)}, f32[3,3,1,2,128]{4,3,2,1,0:T(2,128)S(1)}, u32[]{:S(2)}, u32[]{:S(2)}) collective-permute-start(f32[3,3,1,2,128]{4,3,2,1,0:T(2,128)S(1)} %slice.876), channel_id=1, source_target_pairs={{0,224},{32,0},{64,32},{96,64},{128,96},{160,128},{192,160},{224,1... | collective-permute-start | bytes 27656 | tf_op jit(solution)/shard_map/ppermute | solution.py:27
  157.9 11.4 %collective-permute-start.30 = (f32[3,3,1,2,128]{4,3,2,1,0:T(2,128)S(1)}, f32[3,3,1,2,128]{4,3,2,1,0:T(2,128)S(1)}, u32[]{:S(2)}, u32[]{:S(2)}) collective-permute-start(f32[3,3,1,2,128]{4,3,2,1,0:T(2,128)S(1)} %slice.875), channel_id=1, source_target_pairs={{0,32},{32,64},{64,96},{96,128},{128,160},{160,192},{192,224},{224... | collective-permute-start | bytes 27656 | tf_op jit(solution)/shard_map/ppermute | solution.py:27
  158.2 9.4 %collective-permute-start.34 = (f32[3,3,2,2,1]{4,0,3,2,1:T(4,128)S(1)}, f32[3,3,2,2,1]{4,0,3,2,1:T(4,128)S(1)}, u32[]{:S(2)}, u32[]{:S(2)}) collective-permute-start(f32[3,3,2,2,1]{4,0,3,2,1:T(4,128)S(1)} %slice.883), channel_id=1, source_target_pairs={{0,1},{1,2},{2,3},{3,4},{4,5},{5,6},{6,7},{7,0},{8,9},{9,10},{10,1... | collective-permute-start | bytes 440 | tf_op jit(solution)/shard_map/ppermute | solution.py:27
  158.7 9.0 %collective-permute-start.35 = (f32[3,3,2,2,1]{4,0,3,2,1:T(4,128)S(1)}, f32[3,3,2,2,1]{4,0,3,2,1:T(4,128)S(1)}, u32[]{:S(2)}, u32[]{:S(2)}) collective-permute-start(f32[3,3,2,2,1]{4,0,3,2,1:T(4,128)S(1)} %bitcast.1070), channel_id=1, source_target_pairs={{0,7},{1,0},{2,1},{3,2},{4,3},{5,4},{6,5},{7,6},{8,15},{9,8},{10,9... | collective-permute-start | bytes 440 | tf_op jit(solution)/shard_map/ppermute | solution.py:27
  174.1 13.4 %collective-permute-start.37 = (f32[3,3,1,2,128]{4,3,2,1,0:T(2,128)S(1)}, f32[3,3,1,2,128]{4,3,2,1,0:T(2,128)S(1)}, u32[]{:S(2)}, u32[]{:S(2)}) collective-permute-start(f32[3,3,1,2,128]{4,3,2,1,0:T(2,128)S(1)} %slice.888), channel_id=1, source_target_pairs={{0,224},{32,0},{64,32},{96,64},{128,96},{160,128},{192,160},{224,1... | collective-permute-start | bytes 27656 | tf_op jit(solution)/shard_map/ppermute | solution.py:27
  176.6 10.9 %collective-permute-start.36 = (f32[3,3,1,2,128]{4,3,2,1,0:T(2,128)S(1)}, f32[3,3,1,2,128]{4,3,2,1,0:T(2,128)S(1)}, u32[]{:S(2)}, u32[]{:S(2)}) collective-permute-start(f32[3,3,1,2,128]{4,3,2,1,0:T(2,128)S(1)} %slice.887), channel_id=1, source_target_pairs={{0,32},{32,64},{64,96},{96,128},{128,160},{160,192},{192,224},{224... | collective-permute-start | bytes 27656 | tf_op jit(solution)/shard_map/ppermute | solution.py:27
  177.1 8.7 %collective-permute-start.40 = (f32[3,3,2,2,1]{4,0,3,2,1:T(4,128)S(1)}, f32[3,3,2,2,1]{4,0,3,2,1:T(4,128)S(1)}, u32[]{:S(2)}, u32[]{:S(2)}) collective-permute-start(f32[3,3,2,2,1]{4,0,3,2,1:T(4,128)S(1)} %slice.895), channel_id=1, source_target_pairs={{0,1},{1,2},{2,3},{3,4},{4,5},{5,6},{6,7},{7,0},{8,9},{9,10},{10,1... | collective-permute-start | bytes 440 | tf_op jit(solution)/shard_map/ppermute | solution.py:27
  177.9 7.9 %collective-permute-start.41 = (f32[3,3,2,2,1]{4,0,3,2,1:T(4,128)S(1)}, f32[3,3,2,2,1]{4,0,3,2,1:T(4,128)S(1)}, u32[]{:S(2)}, u32[]{:S(2)}) collective-permute-start(f32[3,3,2,2,1]{4,0,3,2,1:T(4,128)S(1)} %bitcast.1072), channel_id=1, source_target_pairs={{0,7},{1,0},{2,1},{3,2},{4,3},{5,4},{6,5},{7,6},{8,15},{9,8},{10,9... | collective-permute-start | bytes 440 | tf_op jit(solution)/shard_map/ppermute | solution.py:27
  192.2 47.1 %collective-permute-start.43 = (f32[3,3,1,2,128]{4,3,2,1,0:T(2,128)S(1)}, f32[3,3,1,2,128]{4,3,2,1,0:T(2,128)S(1)}, u32[]{:S(2)}, u32[]{:S(2)}) collective-permute-start(f32[3,3,1,2,128]{4,3,2,1,0:T(2,128)S(1)} %slice.900), channel_id=1, source_target_pairs={{0,224},{32,0},{64,32},{96,64},{128,96},{160,128},{192,160},{224,1... | collective-permute-start | bytes 27656 | tf_op jit(solution)/shard_map/ppermute | solution.py:27
  195.7 43.6 %collective-permute-start.42 = (f32[3,3,1,2,128]{4,3,2,1,0:T(2,128)S(1)}, f32[3,3,1,2,128]{4,3,2,1,0:T(2,128)S(1)}, u32[]{:S(2)}, u32[]{:S(2)}) collective-permute-start(f32[3,3,1,2,128]{4,3,2,1,0:T(2,128)S(1)} %slice.899), channel_id=1, source_target_pairs={{0,32},{32,64},{64,96},{96,128},{128,160},{160,192},{192,224},{224... | collective-permute-start | bytes 27656 | tf_op jit(solution)/shard_map/ppermute | solution.py:27
  196.0 8.7 %collective-permute-start.46 = (f32[3,3,2,2,1]{4,0,3,2,1:T(4,128)S(1)}, f32[3,3,2,2,1]{4,0,3,2,1:T(4,128)S(1)}, u32[]{:S(2)}, u32[]{:S(2)}) collective-permute-start(f32[3,3,2,2,1]{4,0,3,2,1:T(4,128)S(1)} %slice.907), channel_id=1, source_target_pairs={{0,1},{1,2},{2,3},{3,4},{4,5},{5,6},{6,7},{7,0},{8,9},{9,10},{10,1... | collective-permute-start | bytes 440 | tf_op jit(solution)/shard_map/ppermute | solution.py:27
  204.8 34.6 %collective-permute-start.45 = (f32[3,3,2,1,128]{4,0,3,2,1:T(4,128)S(1)}, f32[3,3,2,1,128]{4,0,3,2,1:T(4,128)S(1)}, u32[]{:S(2)}, u32[]{:S(2)}) collective-permute-start(f32[3,3,2,1,128]{4,0,3,2,1:T(4,128)S(1)} %slice.904), channel_id=1, source_target_pairs={{0,24},{8,0},{16,8},{24,16},{1,25},{9,1},{17,9},{25,17},{2,26},{10... | collective-permute-start | bytes 27656 | tf_op jit(solution)/shard_map/ppermute | solution.py:27
  204.8 34.6 %collective-permute-start.44 = (f32[3,3,2,1,128]{4,0,3,2,1:T(4,128)S(1)}, f32[3,3,2,1,128]{4,0,3,2,1:T(4,128)S(1)}, u32[]{:S(2)}, u32[]{:S(2)}) collective-permute-start(f32[3,3,2,1,128]{4,0,3,2,1:T(4,128)S(1)} %slice.903), channel_id=1, source_target_pairs={{0,8},{8,16},{16,24},{24,0},{1,9},{9,17},{17,25},{25,1},{2,10},{10... | collective-permute-start | bytes 27656 | tf_op jit(solution)/shard_map/ppermute | solution.py:27
  206.4 8.4 %collective-permute-start.56 = (f32[3,7,7,1]{3,2,1,0:T(8,128)S(1)}, f32[3,7,7,1]{3,2,1,0:T(8,128)S(1)}, u32[]{:S(2)}, u32[]{:S(2)}) collective-permute-start(f32[3,7,7,1]{3,2,1,0:T(8,128)S(1)} %pad_maximum_fusion.11), channel_id=1, source_target_pairs={{0,7},{1,0},{2,1},{3,2},{4,3},{5,4},{6,5},{7,6},{8,15},{9,8},{10,9... | collective-permute-start | bytes 1772 | tf_op jit(solution)/shard_map/ppermute | solution.py:27
  242.0 16.8 %collective-permute-start.49 = (f32[3,3,1,2,128]{4,3,2,1,0:T(2,128)S(1)}, f32[3,3,1,2,128]{4,3,2,1,0:T(2,128)S(1)}, u32[]{:S(2)}, u32[]{:S(2)}) collective-permute-start(f32[3,3,1,2,128]{4,3,2,1,0:T(2,128)S(1)} %slice.912), channel_id=1, source_target_pairs={{0,224},{32,0},{64,32},{96,64},{128,96},{160,128},{192,160},{224,1... | collective-permute-start | bytes 27656 | tf_op jit(solution)/shard_map/ppermute | solution.py:27
  245.0 13.7 %collective-permute-start.48 = (f32[3,3,1,2,128]{4,3,2,1,0:T(2,128)S(1)}, f32[3,3,1,2,128]{4,3,2,1,0:T(2,128)S(1)}, u32[]{:S(2)}, u32[]{:S(2)}) collective-permute-start(f32[3,3,1,2,128]{4,3,2,1,0:T(2,128)S(1)} %slice.911), channel_id=1, source_target_pairs={{0,32},{32,64},{64,96},{96,128},{128,160},{160,192},{192,224},{224... | collective-permute-start | bytes 27656 | tf_op jit(solution)/shard_map/ppermute | solution.py:27
  245.0 13.8 %collective-permute-start.51 = (f32[3,3,2,1,128]{4,0,3,2,1:T(4,128)S(1)}, f32[3,3,2,1,128]{4,0,3,2,1:T(4,128)S(1)}, u32[]{:S(2)}, u32[]{:S(2)}) collective-permute-start(f32[3,3,2,1,128]{4,0,3,2,1:T(4,128)S(1)} %slice.916), channel_id=1, source_target_pairs={{0,24},{8,0},{16,8},{24,16},{1,25},{9,1},{17,9},{25,17},{2,26},{10... | collective-permute-start | bytes 27656 | tf_op jit(solution)/shard_map/ppermute | solution.py:27
  247.6 9.4 %collective-permute-start.52 = (f32[3,3,2,2,1]{4,0,3,2,1:T(4,128)S(1)}, f32[3,3,2,2,1]{4,0,3,2,1:T(4,128)S(1)}, u32[]{:S(2)}, u32[]{:S(2)}) collective-permute-start(f32[3,3,2,2,1]{4,0,3,2,1:T(4,128)S(1)} %slice.919), channel_id=1, source_target_pairs={{0,1},{1,2},{2,3},{3,4},{4,5},{5,6},{6,7},{7,0},{8,9},{9,10},{10,1... | collective-permute-start | bytes 440 | tf_op jit(solution)/shard_map/ppermute | solution.py:27
  251.6 7.0 %collective-permute-start.53 = (f32[3,3,2,2,1]{4,0,3,2,1:T(4,128)S(1)}, f32[3,3,2,2,1]{4,0,3,2,1:T(4,128)S(1)}, u32[]{:S(2)}, u32[]{:S(2)}) collective-permute-start(f32[3,3,2,2,1]{4,0,3,2,1:T(4,128)S(1)} %bitcast.1066), channel_id=1, source_target_pairs={{0,7},{1,0},{2,1},{3,2},{4,3},{5,4},{6,5},{7,6},{8,15},{9,8},{10,9... | collective-permute-start | bytes 440 | tf_op jit(solution)/shard_map/ppermute | solution.py:27
  314.8 9.3 %collective-permute-start.59 = (f32[3,6,6,1]{3,1,2,0:T(8,128)S(1)}, f32[3,6,6,1]{3,1,2,0:T(8,128)S(1)}, u32[]{:S(2)}, u32[]{:S(2)}) collective-permute-start(f32[3,6,6,1]{3,1,2,0:T(8,128)S(1)} %slice.949), channel_id=1, source_target_pairs={{0,1},{1,2},{2,3},{3,4},{4,5},{5,6},{6,7},{7,0},{8,9},{9,10},{10,1... | collective-permute-start | bytes 1304 | tf_op jit(solution)/shard_map/ppermute | solution.py:27
  368.5 8.4 %collective-permute-start.60 = (f32[3,1,6,384]{3,1,2,0:T(1,128)S(1)}, f32[3,1,6,384]{3,1,2,0:T(1,128)S(1)}, u32[]{:S(2)}, u32[]{:S(2)}) collective-permute-start(f32[3,1,6,384]{3,1,2,0:T(1,128)S(1)} %slice.951), channel_id=1, source_target_pairs={{0,224},{32,0},{64,32},{96,64},{128,96},{160,128},{192,160},{224,1... | collective-permute-start | bytes 82952 | tf_op jit(solution)/shard_map/ppermute | solution.py:27
  380.0 9.4 %collective-permute-start.62 = (f32[3,7,7,1]{3,1,2,0:T(8,128)S(1)}, f32[3,7,7,1]{3,1,2,0:T(8,128)S(1)}, u32[]{:S(2)}, u32[]{:S(2)}) collective-permute-start(f32[3,7,7,1]{3,1,2,0:T(8,128)S(1)} %pad_maximum_fusion.9), channel_id=1, source_target_pairs={{0,7},{1,0},{2,1},{3,2},{4,3},{5,4},{6,5},{7,6},{8,15},{9,8},{10,9... | collective-permute-start | bytes 1772 | tf_op jit(solution)/shard_map/ppermute | solution.py:27
  (27 other events, 116.8 us)
where the time goes:
time: 465 us; the launch traced here: 456 us
  starting transfers between devices  149 us (32%)
  blocking collectives  122 us (26%)
  local copies, waits for them, and re-layouts  74 us (16%)
  waiting for transfers between devices  54.4 us (12%)
  matrix products  42 us (9%)
  other arithmetic  8.4 us (2%)
  between operations  5.77 us (1%)
    ppermute x57, starting transfers between devices, passed_along(): return lax.ppermute(x, axis, [(i, (i + by) % count) for i in range(count)])  136 us
    psum x10, blocking collectives, one_axis_at_a_time_2(): x = lax.psum(x, axis)  81.3 us
    ppermute x57, waiting for transfers between devices, passed_along(): return lax.ppermute(x, axis, [(i, (i + by) % count) for i in range(count)])  48.8 us
    pmax x5, blocking collectives, one_axis_at_a_time(): x = lax.pmax(x, axis)  40.6 us
    pad x12, local copies, waits for them, and re-layouts, pad_one(): return lax.pad(operand, jnp.zeros((), operand.dtype), config)  33.2 us
    slice x12, local copies, waits for them, and re-layouts, element_corners(): lax.slice_in_dim(gathered, node_offset, node_offset + 3 * extent - 2, str...  31.8 us
    dot_general x51, matrix products, contract(): jnp.tensordot(as_table(weights_table), operand, axes=([1], [along]), prec...  29.6 us
    dot_general x48, matrix products, trace_along(): jnp.tensordot(as_table(vector), modal_coefficients, axes=([0], [direction...  12.5 us
  transfers between devices with their start and end apart: 63, of which 28 were waited for; matrix products, arithmetic and copies ran while one was open for 10% of the time, Pallas kernels for 0%

commit v1 on v0

v1 whole, which is shorter than its diff:
```python
import functools

import jax
import jax.numpy as jnp
import numpy as np
from jax import lax
from jax.experimental import pallas as pl
from jax.experimental.pallas import tpu as pltpu
from jax.sharding import PartitionSpec as P

MESH = pl.DeviceIdType.MESH
ROUNDS = 4
C0, C1, C2 = 0.7071067811865476, 1.224744871391589, 1.5811388300841898
ROOT3, ROOT15 = 1.7320508075688772, 3.872983346207417
FACE = C0 * C0 + C1 * C1 + C2 * C2
COURANT = 0.1
THETA = 0.3
TRIAL = 0.05
F32 = jnp.float32
BF16 = jnp.bfloat16


def tables():
    points = np.array(
        [-0.8611363115940526, -0.3399810435848563, 0.3399810435848563, 0.8611363115940526]
    )
    weights = 0.5 * np.array(
        [0.3478548451374538, 0.6521451548625461, 0.6521451548625461, 0.3478548451374538]
    )
    centred = points
    points = 0.5 * (points + 1.0)
    nodes = np.array([0.0, 1.0 / 3.0, 2.0 / 3.0, 1.0])
    value = np.zeros((4, 4))
    slope = np.zeros((4, 4))
    for column in range(4):
        others = [nodes[m] for m in range(4) if m != column]
        below = np.prod([nodes[column] - m for m in others])
        for row in range(4):
            t = points[row]
            value[row, column] = np.prod([t - m for m in others]) / below
            slope[row, column] = (
                sum(np.prod([t - others[i] for i in range(3) if i != k]) for k in range(3)) / below
            )
    legendre = np.stack(
        [np.full(4, C0), C1 * centred, C2 * 0.5 * (3.0 * centred**2 - 1.0)], axis=1
    )
    cube = np.einsum("p,q,r->pqr", weights, weights, weights).reshape(64)
    wide = np.zeros((2, 2, 3, 4, 4, 4, 4, 7, 8))
    for x in range(2):
        for y in range(2):
            for d in range(3):
                t = [slope if d == axis else value for axis in range(3)]
                wide[x, y, d, :, :, :, :, 3 * x : 3 * x + 4, 3 * y : 3 * y + 4] = np.einsum(
                    "pi,qj,rk->pqrkij", t[0], t[1], t[2]
                )
    wide = wide.reshape(768, 224)
    return legendre, cube, wide


def halves(a):
    hi = np.asarray(a, np.float32).astype(jnp.bfloat16)
    lo = (np.asarray(a, np.float64) - hi.astype(np.float64)).astype(jnp.bfloat16)
    return hi, lo


def split(x):
    hi = x.astype(BF16)
    return hi, (x - hi.astype(F32)).astype(BF16)


def dot(a, b):
    return lax.dot_general(a, b, (((1,), (0,)), ((), ())), preferred_element_type=F32)


def roll(x, by, axis):
    by %= x.shape[axis]
    return x if by == 0 else pltpu.roll(x, by, axis)


def take(ref, d, i):
    return ref[i] if d == 0 else (ref[:, i] if d == 1 else ref[:, :, i])


def kernel(
    nx,
    ny,
    nz,
    disp_ref,
    modes_ref,
    vel_ref,
    wf_any,
    wb_any,
    perm_any,
    cube_ref,
    adv_ref,
    grad_ref,
    checks_ref,
    wf_ref,
    wb_ref,
    perm_ref,
    term,
    vel,
    zs_out,
    zs_in,
    face_out,
    face_in,
    diag_out,
    diag_in,
    tx_out,
    tx_in,
    ty_out,
    ty_in,
    td_out,
    td_in,
    din,
    t0,
    t1,
    nf,
    jac,
    s_ref,
    om_ref,
    q_ref,
    gh,
    gl,
    pg,
    gx_out,
    gx_in,
    gy_out,
    gy_in,
    gd_out,
    gd_in,
    nt,
    hh,
    max_a,
    max_b,
    sum_a,
    sum_b,
    acc_ref,
    local_sem,
    z_sem,
    face_sem,
    diag_sem,
    t_sem,
    g_sem,
    red_sem,
):
    gx, gy, gz = lax.axis_index("gx"), lax.axis_index("gy"), lax.axis_index("gz")

    def at(dx, dy, dz=0):
        return (
            lax.rem(gx + (dx + nx), nx) if dx else gx,
            lax.rem(gy + (dy + ny), ny) if dy else gy,
            lax.rem(gz + (dz + nz), nz) if dz else gz,
        )

    half = nz // 2
    group_a = [
        (i * half + j, (gx, lax.rem(gy + i, ny), lax.rem(gz + 2 * j, nz)))
        for i in range(ny)
        for j in range(half)
        if (i, j) != (0, 0)
    ]
    flipped = gz + 1 - 2 * lax.rem(gz, 2)
    group_b = [
        (i * 2 + b, (lax.rem(gx + i, nx), gy, flipped if b else gz))
        for i in range(nx)
        for b in range(2)
        if (i, b) != (0, 0)
    ]
    count_a, count_b = ny * half, 2 * nx
    corners = ((1, 1), (1, -1), (-1, 1), (-1, -1))
    sides = ((1, 0), (-1, 0), (0, 1), (0, -1))
    partners = [at(*s) for s in sides + corners] + [at(0, 0, 1), at(0, 0, -1)]
    partners += [p for _, p in group_a] + [p for _, p in group_b]

    barrier = pltpu.get_barrier_semaphore()
    for p in partners:
        pl.semaphore_signal(barrier, inc=1, device_id=p, device_id_type=MESH)

    loads = [
        pltpu.make_async_copy(a, b, local_sem.at[i])
        for i, (a, b) in enumerate(((perm_any, perm_ref), (wf_any, wf_ref), (wb_any, wb_ref)))
    ]
    for c in loads:
        c.start()

    pending = []

    def remote(src, dst, send, recv, to):
        c = pltpu.make_async_remote_copy(
            src_ref=src, dst_ref=dst, send_sem=send, recv_sem=recv, device_id=to, device_id_type=MESH
        )
        c.start()
        pending.append(c)
        return c

    row = lax.broadcasted_iota(jnp.int32, (8, 128), 0)
    lane = lax.broadcasted_iota(jnp.int32, (8, 128), 1)
    xlow = ((row // 2) % 2) == 0
    ylow = (row % 2) == 0
    top = row < 4

    term[0] = jnp.zeros((3, 3, 3, 8, 128), F32)
    vel[...] = jnp.zeros((3, 8, 128), F32)
    for a in range(3):
        for b in range(3):
            for c in range(3):
                term[0, a, b, c, 0:4, :] = modes_ref[a * 9 + b * 3 + c]
        vel[a, 0:4, :] = vel_ref[a]
    speed = jnp.abs(vel[0]) + jnp.abs(vel[1]) + jnp.abs(vel[2])
    fastest = jnp.max(jnp.max(speed, axis=1, keepdims=True), axis=0, keepdims=True)
    max_a[0] = jnp.broadcast_to(fastest, (1, 128))

    def packed_of(i):
        lo = term[0, (2 * i) // 9, (2 * i) // 3 % 3, (2 * i) % 3] if 2 * i < 27 else vel[2 * i - 27]
        j = 2 * i + 1
        hi = term[0, j // 9, j // 3 % 3, j % 3] if j < 27 else vel[j - 27]
        return jnp.where(top, lo, roll(hi, 4, 0))

    for v in range(2):
        low = jnp.zeros((8, 128), F32)
        high = jnp.zeros((8, 128), F32)
        for i in range(8 * v, min(8 * v + 8, 15)):
            q = i % 8
            w = packed_of(i)
            mine = (lane >= 16 * q) & (lane < 16 * q + 16)
            low = jnp.where(mine, roll(w, 16 * q, 1), low)
            high = jnp.where(mine, roll(w, 16 * q + 16, 1), high)
        zs_out[0, v] = low
        zs_out[1, v] = high

    din[...] = jnp.zeros((144, 384), F32)
    for c in range(3):
        for x in range(6):
            din[(c * 6 + x) * 8 : (c * 6 + x) * 8 + 6, :] = disp_ref[c, x]
    whole = din[...]
    hi = whole.astype(BF16)
    rest = whole - hi.astype(F32)
    mid = rest.astype(BF16)
    lo = (rest - mid.astype(F32)).astype(BF16)
    loads[0].wait()
    perm = perm_ref[...]
    din[...] = dot(hi, perm) + (dot(mid, perm) + dot(lo, perm))
    t0[...] = jnp.zeros((504, 128), F32)
    low = jnp.zeros((8, 128), F32)
    high = jnp.zeros((8, 128), F32)
    for k in range(3):
        for c in range(3):
            for x in range(6):
                t = k * 3 + c
                j = t * 6 + x
                piece = din[(c * 6 + x) * 8 : (c * 6 + x) * 8 + 8, k * 128 : k * 128 + 128]
                t0[t * 56 + x * 8 : t * 56 + x * 8 + 8, :] = piece
                mine = (lane >= 2 * j) & (lane < 2 * j + 2)
                low = jnp.where(mine, roll(piece, 2 * j, 1), low)
                high = jnp.where(mine, roll(piece, 2 * j + 2, 1), high)
    zs_out[0, 2] = low
    zs_out[1, 2] = high

    pl.semaphore_wait(barrier, len(partners))

    z_up = remote(zs_out.at[1], zs_in.at[1], z_sem.at[0], z_sem.at[1], at(0, 0, 1))
    z_down = remote(zs_out.at[0], zs_in.at[0], z_sem.at[2], z_sem.at[3], at(0, 0, -1))
    maxes_a = [
        remote(max_a.at[0], max_a.at[s], red_sem.at[0, 0, s], red_sem.at[0, 1, s], p)
        for s, p in group_a
    ]
    z_up.wait_recv()
    z_down.wait_recv()
    for v in range(2):
        from_low = zs_in[1, v]
        from_high = zs_in[0, v]
        for i in range(8 * v, min(8 * v + 8, 15)):
            q = i % 8
            near = jnp.where(
                lane < 16,
                roll(from_high, 128 - 16 * q, 1),
                jnp.where(lane >= 112, roll(from_low, 112 - 16 * q, 1), 0.0),
            )
            for j, part in ((2 * i, roll(near, 4, 0)), (2 * i + 1, near)):
                if j < 27:
                    old = term[0, j // 9, j // 3 % 3, j % 3]
                    term[0, j // 9, j // 3 % 3, j % 3] = jnp.where(top, old, part)
                else:
                    vel[j - 27] = jnp.where(top, vel[j - 27], part)

    def zprev(x):
        axis = x.ndim - 1
        r = roll(x, 1, axis)
        return jnp.where(lane == 0, roll(r, 4, axis - 1), r)

    def znext(x):
        axis = x.ndim - 1
        r = roll(x, 127, axis)
        return jnp.where(lane == 127, roll(r, 4, axis - 1), r)

    v0, v1, v2 = vel[0], vel[1], vel[2]
    zero = jnp.zeros((8, 128), F32)
    inner = (
        jnp.where(xlow, 0.0, COURANT * (v0 + roll(v0, 2, 0))),
        jnp.where(ylow, 0.0, COURANT * (v1 + roll(v1, 1, 0))),
        COURANT * (v2 + zprev(v2)),
    )
    plus = [jnp.maximum(f, 0.0) for f in inner]
    minus = [jnp.minimum(f, 0.0) for f in inner]
    grow1 = [(2.0 * COURANT * ROOT3) * v for v in (v0, v1, v2)]
    grow2 = [(2.0 * COURANT * ROOT15) * v for v in (v0, v1, v2)]
    lows = (xlow, ylow)
    signs = (jnp.where(xlow, 1.0, -1.0), jnp.where(ylow, 1.0, -1.0))

    def outward(parts, d):
        e = C0 * parts[0] + C2 * parts[2]
        o = C1 * parts[1]
        return jnp.where(lows[d], e - o, e + o)

    def local_rate(src, dst):
        rims = []
        for d in range(3):
            u0, u1, u2 = take(src, d, 0), take(src, d, 1), take(src, d, 2)
            e = C0 * u0 + C2 * u2
            o = C1 * u1
            tp = e + o
            tm = e - o
            if d < 2:
                rims.append(jnp.where(lows[d], tm, tp))
                by = 2 - d
                lower = plus[d] * roll(tp, by, 2) + minus[d] * tm
                upper = roll(lower, 8 - by, 2)
            else:
                lower = plus[d] * zprev(tp) + minus[d] * tm
                upper = znext(lower)
            drop = lower - upper
            outs = (
                C0 * drop,
                grow1[d] * u0 - C1 * (lower + upper),
                grow2[d] * u1 + C2 * drop,
            )
            for i in range(3):
                if d == 0:
                    dst[i] = outs[i]
                elif d == 1:
                    dst[:, i] = dst[:, i] + outs[i]
                else:
                    dst[:, :, i] = dst[:, :, i] + outs[i]
        return rims

    def add_face(dst, d, flux):
        signed = signs[d] * flux
        outs = (C0 * signed, -C1 * flux, C2 * signed)
        for i in range(3):
            if d == 0:
                dst[i] = dst[i] + outs[i]
            else:
                dst[:, i] = dst[:, i] + outs[i]

    def sides_of(f, d):
        p, m = jnp.maximum(f, 0.0), jnp.minimum(f, 0.0)
        return jnp.where(lows[d], p, m), jnp.where(lows[d], m, p)

    def meet(a, b, d):
        by = 2 - d
        return jnp.where(lows[d], roll(a, 8 - by, a.ndim - 2), roll(b, by, b.ndim - 2))

    def corner_of(r):
        e = [roll(diag_in[r, i], by, 1) for i, by in enumerate((5, 7, 1, 3))]
        return jnp.where(xlow, jnp.where(ylow, e[0], e[1]), jnp.where(ylow, e[2], e[3]))

    speeds = {}

    def advance(r, hidden):
        src, mid_ref, dst = term.at[2 * r], term.at[2 * r + 1], term.at[2 * r + 2]
        rims = local_rate(src, mid_ref)
        n = 11 if r == 0 else 9
        m = 5 if r == 0 else 3
        for d in range(2):
            by = 2 - d
            far = outward([take(mid_ref, d, i) for i in range(3)], d)
            up = jnp.where(lows[d], roll(far, 8 - by, 2), rims[d])
            down = jnp.where(lows[d], rims[d], roll(far, by, 2))
            for i in range(3):
                face_out[r, 2 * d, 3 * i : 3 * i + 3] = up[i]
                face_out[r, 2 * d + 1, 3 * i : 3 * i + 3] = down[i]
            if r == 0:
                for w in range(2):
                    face_out[r, 2 * d + w, 9] = v0
                    face_out[r, 2 * d + w, 10] = v1
        diag_out[r, 0:3] = outward([rims[0][0], rims[0][1], rims[0][2]], 1)
        if r == 0:
            diag_out[r, 3] = v0
            diag_out[r, 4] = v1
        copies = [
            remote(
                diag_out.at[r, pl.ds(0, m)],
                diag_in.at[r, i, pl.ds(0, m)],
                diag_sem.at[r, 0, i],
                diag_sem.at[r, 1, i],
                at(*s),
            )
            for i, s in enumerate(corners)
        ]
        copies += [
            remote(
                face_out.at[r, i, pl.ds(0, n)],
                face_in.at[r, i, pl.ds(0, n)],
                face_sem.at[r, 0, i],
                face_sem.at[r, 1, i],
                at(*s),
            )
            for i, s in enumerate(sides)
        ]
        hidden()
        for c in copies:
            c.wait_recv()
        if r == 0:
            corner = corner_of(0)
            cv0, cv1 = corner[3], corner[4]
            beside = [meet(face_in[0, 2 * d, 9:11], face_in[0, 2 * d + 1, 9:11], d) for d in (0, 1)]
            speeds["rim"] = (
                sides_of(COURANT * (v0 + beside[0][0]), 0),
                sides_of(COURANT * (v1 + beside[1][1]), 1),
            )
            speeds["far"] = (
                sides_of(COURANT * (beside[0][1] + cv1), 1),
                sides_of(COURANT * (beside[1][0] + cv0), 0),
            )
            edge = corner[0:3]
        else:
            edge = corner_of(r)[0:3]
        ghosts = []
        for d in range(2):
            a = face_in[r, 2 * d, 0:9].reshape(3, 3, 8, 128)
            b = face_in[r, 2 * d + 1, 0:9].reshape(3, 3, 8, 128)
            ghost = meet(a, b, d)
            partial = jnp.where(lows[d], a, b)
            theirs, own = speeds["rim"][d]
            flux = theirs * ghost + own * rims[d]
            add_face(mid_ref, d, flux)
            other = 1 - d
            beyond, inside = speeds["far"][d]
            side_flux = beyond * edge + inside * outward([ghost[0], ghost[1], ghost[2]], other)
            signed = signs[other] * side_flux
            whole_face = partial - (FACE * signs[d]) * flux
            ghosts.append(
                (
                    whole_face[0] + C0 * signed,
                    whole_face[1] - C1 * side_flux,
                    whole_face[2] + C2 * signed,
                )
            )
        rims = local_rate(mid_ref, dst)
        for d in range(2):
            theirs, own = speeds["rim"][d]
            flux = [theirs * ghosts[d][i] + own * rims[d][i] for i in range(3)]
            for j in range(3):
                signed = signs[d] * flux[j]
                for i, value in enumerate((C0 * signed, -C1 * flux[j], C2 * signed)):
                    if d == 0:
                        dst[i, j] = dst[i, j] + value
                    else:
                        dst[j, i] = dst[j, i] + value

    later = {}

    def hidden0():
        tx_out[9] = zs_in[0, 2]
        tx_out[10] = zs_in[1, 2]
        for t in range(9):
            tx_out[t] = t0[t * 56 : t * 56 + 8, :]
        ty_out[...] = jnp.zeros((80, 128), F32)
        ty_out[0:63, :] = t0[pl.ds(0, 63, stride=8), :]
        td_out[...] = jnp.zeros((32, 128), F32)
        td_out[0:9, :] = t0[pl.ds(0, 9, stride=56), :]
        for out, base in ((ty_out, 64), (td_out, 16)):
            out[base : base + 8, :] = zs_in[0, 2]
            out[base + 8 : base + 16, :] = zs_in[1, 2]
        later["t"] = [
            remote(tx_out, tx_in, t_sem.at[0, 0], t_sem.at[1, 0], at(-1, 0)),
            remote(ty_out, ty_in, t_sem.at[0, 1], t_sem.at[1, 1], at(0, -1)),
            remote(td_out, td_in, t_sem.at[0, 2], t_sem.at[1, 2], at(-1, -1)),
        ]
        for c in maxes_a:
            c.wait_recv()
        best = max_a[0]
        for s in range(1, count_a):
            best = jnp.maximum(best, max_a[s])
        max_b[0] = best
        later["max"] = [
            remote(max_b.at[0], max_b.at[s], red_sem.at[1, 0, s], red_sem.at[1, 1, s], p)
            for s, p in group_b
        ]

    def hidden1():
        for c in later["t"]:
            c.wait_recv()
        for t in range(9):
            t0[t * 56 + 48 : t * 56 + 56, :] = tx_in[t]
        t0[pl.ds(6, 63, stride=8), :] = ty_in[0:63, :]
        t0[pl.ds(54, 9, stride=56), :] = td_in[0:9, :]
        packs = []
        for w in range(2):
            own = jnp.where(
                row < 6, zs_in[w, 2], jnp.where(row == 6, roll(ty_in[64 + 8 * w : 72 + 8 * w, :], 6, 0), 0.0)
            )
            rim = jnp.where(
                row < 6, tx_in[9 + w], jnp.where(row == 6, roll(td_in[16 + 8 * w : 24 + 8 * w, :], 6, 0), 0.0)
            )
            packs.append((own, rim))
        for t in range(9):
            for x in range(7):
                j = t * 6 + x % 6
                from_high, from_low = packs[0][x // 6], packs[1][x // 6]
                t1[t * 56 + x * 8 : t * 56 + x * 8 + 8, :] = jnp.where(
                    lane < 2,
                    roll(from_high, 128 - 2 * j, 1),
                    jnp.where(lane >= 126, roll(from_low, 126 - 2 * j, 1), 0.0),
                )
        wide_lane = lax.broadcasted_iota(jnp.int32, (56, 128), 1)
        for c in range(3):
            for k in range(3):
                t = k * 3 + c
                nf[k * 56 : k * 56 + 56, c * 256 : c * 256 + 128] = t0[t * 56 : t * 56 + 56, :]
                nf[k * 56 : k * 56 + 56, c * 256 + 128 : c * 256 + 256] = t1[t * 56 : t * 56 + 56, :]
            a = roll(t0[c * 56 : c * 56 + 56, :], 127, 1)
            b = roll(t1[c * 56 : c * 56 + 56, :], 127, 1)
            nf[168:224, c * 256 : c * 256 + 128] = jnp.where(wide_lane == 127, b, a)
            nf[168:224, c * 256 + 128 : c * 256 + 256] = jnp.where(wide_lane == 127, a, b)

    def hidden2():
        loads[1].wait()
        for c in range(3):
            a, b = split(nf[:, c * 256 : c * 256 + 256])
            jac[:, c * 256 : c * 256 + 256] = (
                dot(wf_ref[0:768, :], a) + dot(wf_ref[768:1536, :], a) + dot(wf_ref[0:768, :], b)
            )

    series = np.polynomial.polynomial.polypow([1.0, 1.0, 0.5], 4)

    def hidden3():
        for c in later["max"]:
            c.wait_recv()
        best = max_b[0]
        for s in range(1, count_b):
            best = jnp.maximum(best, max_b[s])
        tau = jnp.broadcast_to(1.0 / jnp.maximum(best, 0.25), (8, 128))
        acc = float(series[6]) * term[6]
        for k in range(5, -1, -1):
            acc = acc * tau + float(series[k]) * term[k]
        acc_ref[...] = acc
        tau2 = tau * tau
        tau4 = tau2 * tau2
        later["tau"] = (tau4 * tau2 * tau, tau4 * tau4)
        loads[2].wait()

    for r, hidden in enumerate((hidden0, hidden1, hidden2, hidden3)):
        advance(r, hidden)

    legendre, _, _ = tables()
    tau7, tau8 = later["tau"]
    field = acc_ref[...] + ((float(series[7]) * tau7) * term[7] + (float(series[8]) * tau8) * term[8])
    acc_ref[...] = field
    for a in range(3):
        for b in range(3):
            for c in range(3):
                adv_ref[a * 9 + b * 3 + c] = field[a, b, c, 0:4]
    lg = [[float(v) for v in line] for line in legendre]
    for p in range(4):
        along = lg[p][0] * acc_ref[0] + lg[p][1] * acc_ref[1] + lg[p][2] * acc_ref[2]
        for q in range(4):
            second = lg[q][0] * along[0] + lg[q][1] * along[1] + lg[q][2] * along[2]
            for r in range(4):
                g = p * 16 + q * 4 + r
                s_ref[g * 8 : g * 8 + 8, :] = (
                    lg[r][0] * second[0] + lg[r][1] * second[1] + lg[r][2] * second[2]
                )

    pairs = ((0, 0, 1.0), (1, 1, 1.0), (2, 2, 1.0), (0, 1, 2.0), (0, 2, 2.0), (1, 2, 2.0))

    def jacobian(col, g, tile):
        return [
            [
                jac[pl.ds(pl.multiple_of(col * 192 + d * 64 + g * 16, 16), 16), c * 256 + tile * 128 : c * 256 + tile * 128 + 128]
                + (1.0 if c == d else 0.0)
                for d in range(3)
            ]
            for c in range(3)
        ]

    def strain(jm, q):
        a = {}
        for d, e, _ in pairs:
            k = q * (jm[0][d] * jm[0][e] + jm[1][d] * jm[1][e] + jm[2][d] * jm[2][e])
            a[d, e] = a[e, d] = k - 1.0 if d == e else k
        return a

    def inner_product(a, b):
        on = a[0, 0] * b[0, 0] + a[1, 1] * b[1, 1] + a[2, 2] * b[2, 2]
        off = a[0, 1] * b[0, 1] + a[0, 2] * b[0, 2] + a[1, 2] * b[1, 2]
        return on + 2.0 * off

    def forces(step, energy):
        col, g = step // 4, step % 4
        w = cube_ref[pl.ds(pl.multiple_of(g * 16, 16), 16), :]
        for tile in range(2):
            s = s_ref[pl.ds(g * 128 + tile * 4 + col, 16, stride=8), :]
            size = jnp.exp(THETA * s)
            q = jnp.exp((-2.0 * THETA) * s)
            jm = jacobian(col, g, tile)
            a = strain(jm, q)
            if tile == 0:
                om = w * (size * size * size)
                energy = energy + om * inner_product(a, a)
                at_row = pl.ds(pl.multiple_of(col * 64 + g * 16, 16), 16)
                om_ref[at_row, :] = om
                q_ref[at_row, :] = q
            fac = (4.0 * w) * size
            for d in range(3):
                rows = pl.ds(pl.multiple_of(col * 192 + d * 64 + g * 16, 16), 16)
                for c in range(3):
                    value = fac * (jm[c][0] * a[0, d] + jm[c][1] * a[1, d] + jm[c][2] * a[2, d])
                    hi, lo = split(value)
                    gh[rows, c * 256 + tile * 128 : c * 256 + tile * 128 + 128] = hi
                    gl[rows, c * 256 + tile * 128 : c * 256 + tile * 128 + 128] = lo
        return energy

    energy = lax.fori_loop(0, 16, forces, jnp.zeros((16, 128), F32))

    wide_lane = lax.broadcasted_iota(jnp.int32, (56, 128), 1)
    rim = jnp.zeros((56, 128), F32)
    for c in range(3):
        a = gh[:, c * 256 : c * 256 + 256]
        b = gl[:, c * 256 : c * 256 + 256]
        part = dot(wb_ref[0:224, :], a) + dot(wb_ref[224:448, :], a) + dot(wb_ref[0:224, :], b)
        r0 = roll(part[168:224, 0:128], 1, 1)
        r1 = roll(part[168:224, 128:256], 1, 1)
        pg[c * 56 : c * 56 + 56, :] = part[0:56, 0:128] + jnp.where(wide_lane == 0, r1, r0)
        for k in (1, 2):
            pg[(k * 3 + c) * 56 : (k * 3 + c) * 56 + 56, :] = part[k * 56 : k * 56 + 56, 0:128]
        last = part[0:56, 128:256] + r0
        rim = jnp.where(wide_lane == c, roll(last, c, 1), rim)
    pg[504:560, :] = rim

    for t in range(10):
        gx_out[0, t] = pg[t * 56 + 48 : t * 56 + 56, :]
        gx_out[1, t] = pg[t * 56 : t * 56 + 8, :]
    for i, start in enumerate((54, 48, 6, 0)):
        gd_out[i] = jnp.zeros((16, 128), F32)
        gd_out[i, 0:10, :] = pg[pl.ds(start, 10, stride=56), :]
    for i, start in enumerate((6, 0)):
        gy_out[i] = jnp.zeros((72, 128), F32)
        gy_out[i, 0:70, :] = pg[pl.ds(start, 70, stride=8), :]
    moved = [
        remote(gd_out.at[i], gd_in.at[i], g_sem.at[0, 4 + i], g_sem.at[1, 4 + i], at(*s))
        for i, s in enumerate(corners)
    ]
    moved += [
        remote(gx_out.at[i], gx_in.at[i], g_sem.at[0, i], g_sem.at[1, i], at(*sides[i])) for i in range(2)
    ]
    moved += [
        remote(gy_out.at[i], gy_in.at[i], g_sem.at[0, 2 + i], g_sem.at[1, 2 + i], at(*sides[2 + i]))
        for i in range(2)
    ]
    def total(x):
        return jnp.sum(jnp.sum(x, axis=0, keepdims=True), axis=1, keepdims=True)

    energy = total(energy)
    for c in moved:
        c.wait_recv()
    for t in range(10):
        pg[t * 56 : t * 56 + 8, :] = pg[t * 56 : t * 56 + 8, :] + gx_in[0, t]
        pg[t * 56 + 48 : t * 56 + 56, :] = pg[t * 56 + 48 : t * 56 + 56, :] + gx_in[1, t]
    for i, start in enumerate((0, 6)):
        pg[pl.ds(start, 70, stride=8), :] = pg[pl.ds(start, 70, stride=8), :] + gy_in[i, 0:70, :]
    for i, start in enumerate((0, 6, 48, 54)):
        pg[pl.ds(start, 10, stride=56), :] = pg[pl.ds(start, 10, stride=56), :] + gd_in[i, 0:10, :]

    entries = 81.0 * 512.0 * nx * ny * nz
    own = jnp.zeros((8, 128), F32)
    outer = jnp.zeros((8, 128), F32)
    for t in range(10):
        for x in range(7):
            piece = pg[t * 56 + x * 8 : t * 56 + x * 8 + 8, :]
            if t < 9 and x < 6:
                own = own + piece * piece
            else:
                outer = outer + piece * piece
    square = total(jnp.where(row < 6, own, 0.0))
    reach = total(jnp.where(row < 6, outer, own + outer)) + square
    reach_step = TRIAL / jnp.sqrt(1.0 + reach / entries)

    for c in range(3):
        for k in range(3):
            t = k * 3 + c
            nt[k * 56 : k * 56 + 56, c * 128 : c * 128 + 128] = reach_step * pg[t * 56 : t * 56 + 56, :]
        nt[168:224, c * 128 : c * 128 + 128] = reach_step * jnp.where(
            wide_lane == 127, roll(pg[504:560, :], 127 - c, 1), roll(pg[c * 56 : c * 56 + 56, :], 127, 1)
        )
    a, b = split(nt[...])
    hh[...] = dot(wf_ref[0:768, :], a) + dot(wf_ref[768:1536, :], a) + dot(wf_ref[0:768, :], b)

    def coefficients(step, sums):
        col, g = step // 4, step % 4
        at_row = pl.ds(pl.multiple_of(col * 64 + g * 16, 16), 16)
        om, q = om_ref[at_row, :], q_ref[at_row, :]
        jm = jacobian(col, g, 0)
        hm = [
            [
                hh[pl.ds(pl.multiple_of(col * 192 + d * 64 + g * 16, 16), 16), c * 128 : c * 128 + 128]
                for d in range(3)
            ]
            for c in range(3)
        ]
        a = strain(jm, q)
        b, cc = {}, {}
        for d, e, _ in pairs:
            if d == e:
                k = (2.0 * q) * (jm[0][d] * hm[0][d] + jm[1][d] * hm[1][d] + jm[2][d] * hm[2][d])
            else:
                k = q * (
                    (jm[0][d] * hm[0][e] + jm[1][d] * hm[1][e] + jm[2][d] * hm[2][e])
                    + (jm[0][e] * hm[0][d] + jm[1][e] * hm[1][d] + jm[2][e] * hm[2][d])
                )
            b[d, e] = k
            cc[d, e] = q * (hm[0][d] * hm[0][e] + hm[1][d] * hm[1][e] + hm[2][d] * hm[2][e])
        return (
            sums[0] - om * (2.0 * inner_product(a, b)),
            sums[1] + om * (inner_product(b, b) + 2.0 * inner_product(a, cc)),
            sums[2] - om * (2.0 * inner_product(b, cc)),
            sums[3] + om * inner_product(cc, cc),
        )

    none = jnp.zeros((16, 128), F32)
    sums = lax.fori_loop(0, 16, coefficients, (none, none, none, none))
    line = lax.broadcasted_iota(jnp.int32, (1, 128), 1)
    values = [energy, square, reach_step] + [total(s) for s in sums]
    mine = jnp.zeros((1, 128), F32)
    for i, value in enumerate(values):
        mine = jnp.where(line == i, value, mine)
    sum_a[0] = mine
    sums_a = [
        remote(sum_a.at[0], sum_a.at[s], red_sem.at[2, 0, s], red_sem.at[2, 1, s], p)
        for s, p in group_a
    ]

    for c in range(3):
        for x in range(6):
            for k in range(3):
                t = k * 3 + c
                din[(c * 6 + x) * 8 : (c * 6 + x) * 8 + 8, k * 128 : k * 128 + 128] = pg[
                    t * 56 + x * 8 : t * 56 + x * 8 + 8, :
                ]
    whole = din[...]
    hi = whole.astype(BF16)
    rest = whole - hi.astype(F32)
    mid = rest.astype(BF16)
    lo = (rest - mid.astype(F32)).astype(BF16)
    perm = perm_ref[...]

    def back(x):
        return lax.dot_general(x, perm, (((1,), (1,)), ((), ())), preferred_element_type=F32)

    din[...] = back(hi) + (back(mid) + back(lo))
    for c in range(3):
        for x in range(6):
            grad_ref[c, x] = din[(c * 6 + x) * 8 : (c * 6 + x) * 8 + 6, :]

    def weigh(ratio):
        two = ratio * ratio
        return jnp.where(
            line == 3,
            ratio,
            jnp.where(line == 4, two, jnp.where(line == 5, two * ratio, jnp.where(line == 6, two * two, 1.0))),
        )

    def pick(v, i):
        return jnp.sum(jnp.where(line == i, v, 0.0), axis=1, keepdims=True)

    def combine(ref, count):
        steps = [pick(ref[s], 2) for s in range(count)]
        least = functools.reduce(jnp.minimum, steps)
        out = jnp.zeros((1, 128), F32)
        for s in range(count):
            out = out + ref[s] * weigh(least / steps[s])
        return jnp.where(line == 2, least, out)

    for c in sums_a:
        c.wait_recv()
    sum_b[0] = combine(sum_a, count_a)
    sums_b = [
        remote(sum_b.at[0], sum_b.at[s], red_sem.at[3, 0, s], red_sem.at[3, 1, s], p)
        for s, p in group_b
    ]
    for c in sums_b:
        c.wait_recv()
    final = combine(sum_b, count_b)
    square = pick(final, 1)
    step_length = TRIAL / jnp.sqrt(1.0 + square / entries)
    grown = final * weigh(step_length / pick(final, 2))
    elements = 512.0 * nx * ny * nz
    trial = jnp.sum(jnp.where((line == 0) | ((line >= 3) & (line < 7)), grown, 0.0))
    checks_ref[0] = jnp.sum(jnp.where(line == 0, final, 0.0)) * (1.0 / elements)
    checks_ref[1] = jnp.sum(jnp.where(line == 1, final, 0.0)) * (1.0 / entries)
    checks_ref[2] = trial * (1.0 / elements)

    for c in pending:
        c.wait_send()


def solution(mesh):
    nx, ny, nz = mesh.shape["gx"], mesh.shape["gy"], mesh.shape["gz"]
    _, cube, wide = tables()
    hi, lo = halves(wide)
    wf = np.concatenate([hi, lo], axis=0)
    wb = np.concatenate([hi.T, lo.T], axis=0)
    perm = np.zeros((384, 384), np.float32)
    for k in range(3):
        perm[3 * np.arange(128) + k, k * 128 + np.arange(128)] = 1.0
    perm = perm.astype(jnp.bfloat16)
    cube = np.broadcast_to(np.asarray(cube, np.float32)[:, None], (64, 128))
    count_a, count_b = ny * (nz // 2), 2 * nx
    most = max(count_a, count_b)
    vmem = pl.BlockSpec(memory_space=pltpu.VMEM)
    anywhere = pl.BlockSpec(memory_space=pl.ANY)
    dma = pltpu.SemaphoreType.DMA
    call = pl.pallas_call(
        functools.partial(kernel, nx, ny, nz),
        name="tmop_step",
        out_shape=(
            jax.ShapeDtypeStruct((27, 4, 128), F32),
            jax.ShapeDtypeStruct((3, 6, 6, 384), F32),
            jax.ShapeDtypeStruct((3,), F32),
        ),
        in_specs=[vmem, vmem, vmem, anywhere, anywhere, anywhere, vmem],
        out_specs=(vmem, vmem, pl.BlockSpec(memory_space=pltpu.SMEM)),
        scratch_shapes=[
            pltpu.VMEM((1536, 224), BF16),
            pltpu.VMEM((448, 768), BF16),
            pltpu.VMEM((384, 384), BF16),
            pltpu.VMEM((2 * ROUNDS + 1, 3, 3, 3, 8, 128), F32),
            pltpu.VMEM((3, 8, 128), F32),
            pltpu.VMEM((2, 3, 8, 128), F32),
            pltpu.VMEM((2, 3, 8, 128), F32),
            pltpu.VMEM((ROUNDS, 4, 11, 8, 128), F32),
            pltpu.VMEM((ROUNDS, 4, 11, 8, 128), F32),
            pltpu.VMEM((ROUNDS, 5, 8, 128), F32),
            pltpu.VMEM((ROUNDS, 4, 5, 8, 128), F32),
            pltpu.VMEM((11, 8, 128), F32),
            pltpu.VMEM((11, 8, 128), F32),
            pltpu.VMEM((80, 128), F32),
            pltpu.VMEM((80, 128), F32),
            pltpu.VMEM((32, 128), F32),
            pltpu.VMEM((32, 128), F32),
            pltpu.VMEM((144, 384), F32),
            pltpu.VMEM((504, 128), F32),
            pltpu.VMEM((504, 128), F32),
            pltpu.VMEM((224, 768), F32),
            pltpu.VMEM((768, 768), F32),
            pltpu.VMEM((512, 128), F32),
            pltpu.VMEM((256, 128), F32),
            pltpu.VMEM((256, 128), F32),
            pltpu.VMEM((768, 768), BF16),
            pltpu.VMEM((768, 768), BF16),
            pltpu.VMEM((560, 128), F32),
            pltpu.VMEM((2, 10, 8, 128), F32),
            pltpu.VMEM((2, 10, 8, 128), F32),
            pltpu.VMEM((2, 72, 128), F32),
            pltpu.VMEM((2, 72, 128), F32),
            pltpu.VMEM((4, 16, 128), F32),
            pltpu.VMEM((4, 16, 128), F32),
            pltpu.VMEM((224, 384), F32),
            pltpu.VMEM((768, 384), F32),
            pltpu.VMEM((count_a, 1, 128), F32),
            pltpu.VMEM((count_b, 1, 128), F32),
            pltpu.VMEM((count_a, 1, 128), F32),
            pltpu.VMEM((count_b, 1, 128), F32),
            pltpu.VMEM((3, 3, 3, 8, 128), F32),
            dma((3,)),
            dma((4,)),
            dma((ROUNDS, 2, 4)),
            dma((ROUNDS, 2, 4)),
            dma((2, 3)),
            dma((2, 8)),
            dma((4, 2, most)),
        ],
        compiler_params=pltpu.CompilerParams(
            collective_id=0, has_side_effects=True, vmem_limit_bytes=48 * 1024 * 1024
        ),
    )

    def on_device(displacement, size_field_modes, velocity):
        adv, grad, checks = call(
            displacement,
            size_field_modes.reshape(27, 4, 128),
            velocity.reshape(3, 4, 128),
            jnp.asarray(wf),
            jnp.asarray(wb),
            jnp.asarray(perm),
            jnp.asarray(cube),
        )
        return adv.reshape(27, 2, 2, 128), grad, checks

    spec = P(None, "gx", "gy", "gz")
    return jax.shard_map(
        on_device, mesh=mesh, in_specs=(spec, spec, spec), out_specs=(spec, spec, P()), check_vma=False
    )
```

time: 465 us -> 66.8 us (0.14); the launches traced: 456 us -> 66.4 us
  starting transfers between devices: 149 us -> 0 us
  blocking collectives: 122 us -> 0 us
  local copies, waits for them, and re-layouts: 74 us -> 8.1 us
  Pallas kernels: 0 us -> 57.7 us
  waiting for transfers between devices: 54.4 us -> 0 us
  matrix products: 42 us -> 0 us
  other arithmetic: 8.4 us -> 0 us
  between operations: 5.77 us -> 0.65 us
    ppermute x63 -> x0, starting transfers between devices: 149 us -> none  [the longest x57 136 us: passed_along(): return lax.ppermute(x, axis, [(i, (i + by) % count) for i in range(count)])]
    psum x10 -> x0, blocking collectives: 81.3 us -> none  [one_axis_at_a_time_2(): x = lax.psum(x, axis)]
    pallas_call x0 -> x1, Pallas kernels: none -> 57.7 us  [on_device(): call(displacement, size_field_modes.reshape(27, 4, 128), velocity.reshape...]
    ppermute x63 -> x0, waiting for transfers between devices: 54.4 us -> none  [the longest x57 48.8 us: passed_along(): return lax.ppermute(x, axis, [(i, (i + by) % count) for i in range(count)])]
    dot_general x99 -> x0, matrix products: 42 us -> none  [the longest x51 29.6 us: contract(): jnp.tensordot(as_table(weights_table), operand, axes=([1], [along]), prec...]
    pmax x5 -> x0, blocking collectives: 40.6 us -> none  [one_axis_at_a_time(): x = lax.pmax(x, axis)]
    slice x88 -> x0, local copies, waits for them, and re-layouts: 34.8 us -> none  [the longest x12 31.8 us: element_corners(): lax.slice_in_dim(gathered, node_offset, node_offset + 3 * extent - 2, str...]
    pad x12 -> x0, local copies, waits for them, and re-layouts: 33.2 us -> none  [pad_one(): return lax.pad(operand, jnp.zeros((), operand.dtype), config)]
  transfers between devices with their start and end apart: 63 -> 0, of which waited for: 28 -> 0; matrix products, arithmetic and copies ran while one was open for 10% -> 0% of each run, Pallas kernels for 0% -> 0%
where the time goes in v1:
time: 66.8 us; the launch traced here: 66.4 us
  Pallas kernels  57.7 us (86%)
  local copies, waits for them, and re-layouts  8.1 us (12%)
    pallas_call x1, Pallas kernels, on_device(): call(displacement, size_field_modes.reshape(27, 4, 128), velocity.reshape...  57.7 us
    unnamed x17, local copies, waits for them, and re-layouts  8.03 us

profile of v1, /device:TPU:1, one launch (start us, length us, event | category | flops | bytes accessed | tf_op | source)
XLA Modules:
  0.0 66.4 jit_solution(843741909713996475)
XLA Ops:
  0.6 0.0 copy-start.6
  0.6 0.6 copy-done.6
  1.3 0.0 copy-start.5
  1.3 0.1 jit_solution_.3.cube_ref
  1.4 0.6 copy-done.5
  2.0 0.0 copy-start
  2.0 1.1 %copy-done = bf16[1536,224]{1,0:T(8,128)(2,1)S(1)} copy-done((bf16[1536,224]{1,0:T(8,128)(2,1)S(1)}, bf16[1536,224]{1,0:T(8,128)(2,1)}, u32[]{:S(2)}) %copy-start) | copy-done | bytes 688152
  3.1 0.0 copy-start.1
  3.1 1.1 %copy-done.1 = bf16[448,768]{1,0:T(8,128)(2,1)S(1)} copy-done((bf16[448,768]{1,0:T(8,128)(2,1)S(1)}, bf16[448,768]{1,0:T(8,128)(2,1)}, u32[]{:S(2)}) %copy-start.1) | copy-done | bytes 688152
  4.2 0.0 copy-start.2
  4.2 1.0 %copy-done.2 = bf16[384,384]{1,0:T(8,128)(2,1)S(1)} copy-done((bf16[384,384]{1,0:T(8,128)(2,1)S(1)}, bf16[384,384]{1,0:T(8,128)(2,1)}, u32[]{:S(2)}) %copy-start.2) | copy-done | bytes 294936
  5.2 0.0 copy-start.3
  5.2 0.9 %copy-done.3 = f32[3,6,6,384]{3,2,1,0:T(8,128)S(1)} copy-done((f32[3,6,6,384]{3,2,1,0:T(8,128)S(1)}, f32[3,6,6,384]{3,2,1,0:T(8,128)}, u32[]{:S(2)}) %copy-start.3) | copy-done | bytes 165912
  6.1 0.0 copy-start.4
  6.1 0.8 %copy-done.4 = f32[27,2,2,128]{3,2,1,0:T(2,128)S(1)} copy-done((f32[27,2,2,128]{3,2,1,0:T(2,128)S(1)}, f32[27,2,2,128]{3,2,1,0:T(2,128)}, u32[]{:S(2)}) %copy-start.4) | copy-done | bytes 55320
  6.9 57.7 %tmop_step.1 = (f32[27,4,128]{2,1,0:T(4,128)S(1)}, f32[3,6,6,384]{3,2,1,0:T(8,128)S(1)}, f32[3]{0:T(128)S(1)}) custom-call(f32[3,6,6,384]{3,2,1,0:T(8,128)S(1)} %copy-done.3, f32[27,4,128]{2,1,0:T(4,128)S(1)} %bitcast.4, f32[3,4,128]{2,1,0:T(4,128)S(1)} %bitcast.5, bf16[1536,224]{1,0:T(8,128)(2,1)S(1)} %copy-done, bf16[448,768]{1,0:T(8,128)(2,1)S(1)} %copy-done.1, ...), custom_call_target="tpu_custom_call" | custom-call | tf_op jit(solution)/shard_map/tmop_step/pallas_call | solution.py:890
  64.6 0.6 copy.13
  65.2 0.7 %copy.14 = f32[3,6,6,384]{3,2,1,0:T(8,128)} copy(f32[3,6,6,384]{3,2,1,0:T(8,128)S(1)} %get-tuple-element.13) | data formatting | bytes 331776
  65.9 0.5 copy.15
Async XLA Ops:
  0.6 0.7 copy-start.6
  1.3 0.7 %copy-start.5 = (f32[3,2,2,128]{3,2,1,0:T(2,128)S(1)}, f32[3,2,2,128]{3,2,1,0:T(2,128)}, u32[]{:S(2)}) copy-start(f32[3,2,2,128]{3,2,1,0:T(2,128)} %param.9) | copy-start | bytes 18436
  2.0 1.1 %copy-start = (bf16[1536,224]{1,0:T(8,128)(2,1)S(1)}, bf16[1536,224]{1,0:T(8,128)(2,1)}, u32[]{:S(2)}) copy-start(bf16[1536,224]{1,0:T(8,128)(2,1)} %constant.8.clone.wf_any) | copy-start | bytes 2064388
  3.1 1.1 %copy-start.1 = (bf16[448,768]{1,0:T(8,128)(2,1)S(1)}, bf16[448,768]{1,0:T(8,128)(2,1)}, u32[]{:S(2)}) copy-start(bf16[448,768]{1,0:T(8,128)(2,1)} %constant.9.clone.wb_any) | copy-start | bytes 2064388
  4.2 1.0 %copy-start.2 = (bf16[384,384]{1,0:T(8,128)(2,1)S(1)}, bf16[384,384]{1,0:T(8,128)(2,1)}, u32[]{:S(2)}) copy-start(bf16[384,384]{1,0:T(8,128)(2,1)} %constant.10.clone.perm_any) | copy-start | bytes 884740
  5.2 0.9 %copy-start.3 = (f32[3,6,6,384]{3,2,1,0:T(8,128)S(1)}, f32[3,6,6,384]{3,2,1,0:T(8,128)}, u32[]{:S(2)}) copy-start(f32[3,6,6,384]{3,2,1,0:T(8,128)} %disp_ref.1) | copy-start | bytes 497668
  6.1 0.8 %copy-start.4 = (f32[27,2,2,128]{3,2,1,0:T(2,128)S(1)}, f32[27,2,2,128]{3,2,1,0:T(2,128)}, u32[]{:S(2)}) copy-start(f32[27,2,2,128]{3,2,1,0:T(2,128)} %param.8) | copy-start | bytes 165892

commit v2 on v1

--- a/solution.py
+++ b/solution.py
@@ -15,6 +15,7 @@
 FACE = C0 * C0 + C1 * C1 + C2 * C2
 COURANT = 0.1
 THETA = 0.3
+OUTER_WEIGHT, INNER_WEIGHT = 0.5 * 0.3478548451374538, 0.5 * 0.6521451548625461
 TRIAL = 0.05
 F32 = jnp.float32
 BF16 = jnp.bfloat16
@@ -23,9 +24,6 @@
 def tables():
     points = np.array(
         [-0.8611363115940526, -0.3399810435848563, 0.3399810435848563, 0.8611363115940526]
-    )
-    weights = 0.5 * np.array(
-        [0.3478548451374538, 0.6521451548625461, 0.6521451548625461, 0.3478548451374538]
     )
     centred = points
     points = 0.5 * (points + 1.0)
@@ -44,7 +42,6 @@
     legendre = np.stack(
         [np.full(4, C0), C1 * centred, C2 * 0.5 * (3.0 * centred**2 - 1.0)], axis=1
     )
-    cube = np.einsum("p,q,r->pqr", weights, weights, weights).reshape(64)
     wide = np.zeros((2, 2, 3, 4, 4, 4, 4, 7, 8))
     for x in range(2):
         for y in range(2):
@@ -54,7 +51,7 @@
                     "pi,qj,rk->pqrkij", t[0], t[1], t[2]
                 )
     wide = wide.reshape(768, 224)
-    return legendre, cube, wide
+    return legendre, wide
 
 
 def halves(a):
@@ -85,16 +82,21 @@
     nx,
     ny,
     nz,
+    disp_any,
+    modes_any,
+    vel_any,
+    wf_any,
+    wb_any,
+    perm_any,
+    adv_any,
+    grad_any,
+    checks_ref,
+    adv_ref,
+    grad_ref,
     disp_ref,
     modes_ref,
     vel_ref,
-    wf_any,
-    wb_any,
-    perm_any,
     cube_ref,
-    adv_ref,
-    grad_ref,
-    checks_ref,
     wf_ref,
     wb_ref,
     perm_ref,
@@ -135,6 +137,8 @@
     max_b,
     sum_a,
     sum_b,
+    max_c,
+    sum_c,
     acc_ref,
     local_sem,
     z_sem,
@@ -162,16 +166,17 @@
     ]
     flipped = gz + 1 - 2 * lax.rem(gz, 2)
     group_b = [
-        (i * 2 + b, (lax.rem(gx + i, nx), gy, flipped if b else gz))
-        for i in range(nx)
+        (i * 2 + b, (lax.rem(gx + 2 * i, nx), gy, flipped if b else gz))
+        for i in range(nx // 2)
         for b in range(2)
         if (i, b) != (0, 0)
     ]
-    count_a, count_b = ny * half, 2 * nx
+    group_c = [(1, (gx + 1 - 2 * lax.rem(gx, 2), gy, gz))]
+    count_a, count_b, count_c = ny * half, nx, 2
     corners = ((1, 1), (1, -1), (-1, 1), (-1, -1))
     sides = ((1, 0), (-1, 0), (0, 1), (0, -1))
     partners = [at(*s) for s in sides + corners] + [at(0, 0, 1), at(0, 0, -1)]
-    partners += [p for _, p in group_a] + [p for _, p in group_b]
+    partners += [p for _, p in group_a + group_b + group_c]
 
     barrier = pltpu.get_barrier_semaphore()
     for p in partners:
@@ -179,10 +184,19 @@
 
     loads = [
         pltpu.make_async_copy(a, b, local_sem.at[i])
-        for i, (a, b) in enumerate(((perm_any, perm_ref), (wf_any, wf_ref), (wb_any, wb_ref)))
+        for i, (a, b) in enumerate(
+            (
+                (perm_any, perm_ref),
+                (wf_any, wf_ref),
+                (wb_any, wb_ref),
+                (modes_any, modes_ref),
+                (vel_any, vel_ref),
+                (disp_any, disp_ref),
+            )
+        )
     ]
-    for c in loads:
-        c.start()
+    for i in (3, 4, 5, 0, 1, 2):
+        loads[i].start()
 
     pending = []
 
@@ -202,6 +216,13 @@
 
     term[0] = jnp.zeros((3, 3, 3, 8, 128), F32)
     vel[...] = jnp.zeros((3, 8, 128), F32)
+    point = lax.broadcasted_iota(jnp.int32, (64, 128), 0)
+    cube = jnp.ones((64, 128), F32)
+    for place in (point // 16, (point // 4) % 4, point % 4):
+        cube = cube * jnp.where((place == 0) | (place == 3), OUTER_WEIGHT, INNER_WEIGHT)
+    cube_ref[...] = cube
+    loads[3].wait()
+    loads[4].wait()
     for a in range(3):
         for b in range(3):
             for c in range(3):
@@ -230,6 +251,7 @@
         zs_out[1, v] = high
 
     din[...] = jnp.zeros((144, 384), F32)
+    loads[5].wait()
     for c in range(3):
         for x in range(6):
             din[(c * 6 + x) * 8 : (c * 6 + x) * 8 + 6, :] = disp_ref[c, x]
@@ -361,9 +383,26 @@
         by = 2 - d
         return jnp.where(lows[d], roll(a, 8 - by, a.ndim - 2), roll(b, by, b.ndim - 2))
 
-    def corner_of(r):
-        e = [roll(diag_in[r, i], by, 1) for i, by in enumerate((5, 7, 1, 3))]
-        return jnp.where(xlow, jnp.where(ylow, e[0], e[1]), jnp.where(ylow, e[2], e[3]))
+    corner_rows = (3, 2, 1, 0)
+
+    def pack_corner(values, r):
+        tiles = []
+        for base in range(0, len(values), 4):
+            tile = zero
+            for w, value in enumerate(values[base : base + 4]):
+                for h in range(2):
+                    tile = jnp.where(row == 2 * w + h, roll(value, 2 * w + h - 4 * h - r, 0), tile)
+            tiles.append(tile)
+        return tiles
+
+    def corner_of(r, w):
+        out = zero
+        for i, source in enumerate(corner_rows):
+            tile = diag_in[r, i, w // 4]
+            for h in range(2):
+                to = 4 * h + 3 - source
+                out = jnp.where(row == to, roll(tile, to - 2 * (w % 4) - h, 0), out)
+        return out
 
     speeds = {}
 
@@ -371,7 +410,7 @@
         src, mid_ref, dst = term.at[2 * r], term.at[2 * r + 1], term.at[2 * r + 2]
         rims = local_rate(src, mid_ref)
         n = 11 if r == 0 else 9
-        m = 5 if r == 0 else 3
+        m = 2 if r == 0 else 1
         for d in range(2):
             by = 2 - d
             far = outward([take(mid_ref, d, i) for i in range(3)], d)
@@ -384,13 +423,14 @@
                 for w in range(2):
                     face_out[r, 2 * d + w, 9] = v0
                     face_out[r, 2 * d + w, 10] = v1
-        diag_out[r, 0:3] = outward([rims[0][0], rims[0][1], rims[0][2]], 1)
-        if r == 0:
-            diag_out[r, 3] = v0
-            diag_out[r, 4] = v1
-        copies = [
+        edge = outward([rims[0][0], rims[0][1], rims[0][2]], 1)
+        values = [edge[0], edge[1], edge[2]] + ([v0, v1] if r == 0 else [])
+        for i, source in enumerate(corner_rows):
+            for w, tile in enumerate(pack_corner(values, source)):
+                diag_out[r, i, w] = tile
+        corner_copies = [
             remote(
-                diag_out.at[r, pl.ds(0, m)],
+                diag_out.at[r, i, pl.ds(0, m)],
                 diag_in.at[r, i, pl.ds(0, m)],
                 diag_sem.at[r, 0, i],
                 diag_sem.at[r, 1, i],
@@ -398,7 +438,7 @@
             )
             for i, s in enumerate(corners)
         ]
-        copies += [
+        copies = [
             remote(
                 face_out.at[r, i, pl.ds(0, n)],
                 face_in.at[r, i, pl.ds(0, n)],
@@ -412,21 +452,12 @@
         for c in copies:
             c.wait_recv()
         if r == 0:
-            corner = corner_of(0)
-            cv0, cv1 = corner[3], corner[4]
             beside = [meet(face_in[0, 2 * d, 9:11], face_in[0, 2 * d + 1, 9:11], d) for d in (0, 1)]
             speeds["rim"] = (
                 sides_of(COURANT * (v0 + beside[0][0]), 0),
                 sides_of(COURANT * (v1 + beside[1][1]), 1),
             )
-            speeds["far"] = (
-                sides_of(COURANT * (beside[0][1] + cv1), 1),
-                sides_of(COURANT * (beside[1][0] + cv0), 0),
-            )
-            edge = corner[0:3]
-        else:
-            edge = corner_of(r)[0:3]
-        ghosts = []
+        halves_of = []
         for d in range(2):
             a = face_in[r, 2 * d, 0:9].reshape(3, 3, 8, 128)
             b = face_in[r, 2 * d + 1, 0:9].reshape(3, 3, 8, 128)
@@ -435,11 +466,24 @@
             theirs, own = speeds["rim"][d]
             flux = theirs * ghost + own * rims[d]
             add_face(mid_ref, d, flux)
+            near = outward([ghost[0], ghost[1], ghost[2]], 1 - d)
+            halves_of.append((partial - (FACE * signs[d]) * flux, near))
+        for c in corner_copies:
+            c.wait_recv()
+        if r == 0:
+            cv0, cv1 = corner_of(0, 3), corner_of(0, 4)
+            speeds["far"] = (
+                sides_of(COURANT * (beside[0][1] + cv1), 1),
+                sides_of(COURANT * (beside[1][0] + cv0), 0),
+            )
+        edge = jnp.stack([corner_of(r, w) for w in range(3)])
+        ghosts = []
+        for d in range(2):
+            whole_face, near = halves_of[d]
             other = 1 - d
             beyond, inside = speeds["far"][d]
-            side_flux = beyond * edge + inside * outward([ghost[0], ghost[1], ghost[2]], other)
+            side_flux = beyond * edge + inside * near
             signed = signs[other] * side_flux
-            whole_face = partial - (FACE * signs[d]) * flux
             ghosts.append(
                 (
                     whole_face[0] + C0 * signed,
@@ -483,13 +527,20 @@
         best = max_a[0]
         for s in range(1, count_a):
             best = jnp.maximum(best, max_a[s])
-        max_b[0] = best
+        max_c[0] = best
+        later["pair"] = [
+            remote(max_c.at[0], max_c.at[s], red_sem.at[4, 0, s], red_sem.at[4, 1, s], p)
+            for s, p in group_c
+        ]
+
+    def hidden1():
+        for c in later["pair"]:
+            c.wait_recv()
+        max_b[0] = jnp.maximum(max_c[0], max_c[1])
         later["max"] = [
             remote(max_b.at[0], max_b.at[s], red_sem.at[1, 0, s], red_sem.at[1, 1, s], p)
             for s, p in group_b
         ]
-
-    def hidden1():
         for c in later["t"]:
             c.wait_recv()
         for t in range(9):
@@ -554,7 +605,7 @@
     for r, hidden in enumerate((hidden0, hidden1, hidden2, hidden3)):
         advance(r, hidden)
 
-    legendre, _, _ = tables()
+    legendre, _ = tables()
     tau7, tau8 = later["tau"]
     field = acc_ref[...] + ((float(series[7]) * tau7) * term[7] + (float(series[8]) * tau8) * term[8])
     acc_ref[...] = field
@@ -562,6 +613,8 @@
         for b in range(3):
             for c in range(3):
                 adv_ref[a * 9 + b * 3 + c] = field[a, b, c, 0:4]
+    leaving = [pltpu.make_async_copy(adv_ref, adv_any, local_sem.at[6])]
+    leaving[0].start()
     lg = [[float(v) for v in line] for line in legendre]
     for p in range(4):
         along = lg[p][0] * acc_ref[0] + lg[p][1] * acc_ref[1] + lg[p][2] * acc_ref[2]
@@ -762,6 +815,8 @@
     for c in range(3):
         for x in range(6):
             grad_ref[c, x] = din[(c * 6 + x) * 8 : (c * 6 + x) * 8 + 6, :]
+    leaving.append(pltpu.make_async_copy(grad_ref, grad_any, local_sem.at[7]))
+    leaving[1].start()
 
     def weigh(ratio):
         two = ratio * ratio
@@ -784,7 +839,14 @@
 
     for c in sums_a:
         c.wait_recv()
-    sum_b[0] = combine(sum_a, count_a)
+    sum_c[0] = combine(sum_a, count_a)
+    sums_c = [
+        remote(sum_c.at[0], sum_c.at[s], red_sem.at[5, 0, s], red_sem.at[5, 1, s], p)
+        for s, p in group_c
+    ]
+    for c in sums_c:
+        c.wait_recv()
+    sum_b[0] = combine(sum_c, count_c)
     sums_b = [
         remote(sum_b.at[0], sum_b.at[s], red_sem.at[3, 0, s], red_sem.at[3, 1, s], p)
         for s, p in group_b
@@ -803,11 +865,25 @@
 
     for c in pending:
         c.wait_send()
+    for c in leaving:
+        c.wait()
+
+
+def leave_kernel(a, b, c, to_a, to_b, to_c, sem):
+    copies = [
+        pltpu.make_async_copy(x, y, sem.at[i]) for i, (x, y) in enumerate(((a, to_a), (b, to_b)))
+    ]
+    for i in range(3):
+        to_c[i] = c[i]
+    for copy in copies:
+        copy.start()
+    for copy in copies:
+        copy.wait()
 
 
 def solution(mesh):
     nx, ny, nz = mesh.shape["gx"], mesh.shape["gy"], mesh.shape["gz"]
-    _, cube, wide = tables()
+    _, wide = tables()
     hi, lo = halves(wide)
     wf = np.concatenate([hi, lo], axis=0)
     wb = np.concatenate([hi.T, lo.T], axis=0)
@@ -815,11 +891,10 @@
     for k in range(3):
         perm[3 * np.arange(128) + k, k * 128 + np.arange(128)] = 1.0
     perm = perm.astype(jnp.bfloat16)
-    cube = np.broadcast_to(np.asarray(cube, np.float32)[:, None], (64, 128))
-    count_a, count_b = ny * (nz // 2), 2 * nx
+    count_a, count_b = ny * (nz // 2), nx
     most = max(count_a, count_b)
-    vmem = pl.BlockSpec(memory_space=pltpu.VMEM)
     anywhere = pl.BlockSpec(memory_space=pl.ANY)
+    hbm = pl.BlockSpec(memory_space=pltpu.HBM)
     dma = pltpu.SemaphoreType.DMA
     call = pl.pallas_call(
         functools.partial(kernel, nx, ny, nz),
@@ -829,9 +904,15 @@
             jax.ShapeDtypeStruct((3, 6, 6, 384), F32),
             jax.ShapeDtypeStruct((3,), F32),
         ),
-        in_specs=[vmem, vmem, vmem, anywhere, anywhere, anywhere, vmem],
-        out_specs=(vmem, vmem, pl.BlockSpec(memory_space=pltpu.SMEM)),
+        in_specs=[hbm] * 6,
+        out_specs=(hbm, hbm, pl.BlockSpec(memory_space=pltpu.SMEM)),
         scratch_shapes=[
+            pltpu.VMEM((27, 4, 128), F32),
+            pltpu.VMEM((3, 6, 6, 384), F32),
+            pltpu.VMEM((3, 6, 6, 384), F32),
+            pltpu.VMEM((27, 4, 128), F32),
+            pltpu.VMEM((3, 4, 128), F32),
+            pltpu.VMEM((64, 128), F32),
             pltpu.VMEM((1536, 224), BF16),
             pltpu.VMEM((448, 768), BF16),
             pltpu.VMEM((384, 384), BF16),
@@ -841,8 +922,8 @@
             pltpu.VMEM((2, 3, 8, 128), F32),
             pltpu.VMEM((ROUNDS, 4, 11, 8, 128), F32),
             pltpu.VMEM((ROUNDS, 4, 11, 8, 128), F32),
-            pltpu.VMEM((ROUNDS, 5, 8, 128), F32),
-            pltpu.VMEM((ROUNDS, 4, 5, 8, 128), F32),
+            pltpu.VMEM((ROUNDS, 4, 2, 8, 128), F32),
+            pltpu.VMEM((ROUNDS, 4, 2, 8, 128), F32),
             pltpu.VMEM((11, 8, 128), F32),
             pltpu.VMEM((11, 8, 128), F32),
             pltpu.VMEM((80, 128), F32),
@@ -872,18 +953,33 @@
             pltpu.VMEM((count_b, 1, 128), F32),
             pltpu.VMEM((count_a, 1, 128), F32),
             pltpu.VMEM((count_b, 1, 128), F32),
+            pltpu.VMEM((2, 1, 128), F32),
+            pltpu.VMEM((2, 1, 128), F32),
             pltpu.VMEM((3, 3, 3, 8, 128), F32),
-            dma((3,)),
+            dma((8,)),
             dma((4,)),
             dma((ROUNDS, 2, 4)),
             dma((ROUNDS, 2, 4)),
             dma((2, 3)),
             dma((2, 8)),
-            dma((4, 2, most)),
+            dma((6, 2, most)),
         ],
         compiler_params=pltpu.CompilerParams(
-            collective_id=0, has_side_effects=True, vmem_limit_bytes=48 * 1024 * 1024
+            collective_id=0, has_side_effects=True, vmem_limit_bytes=67_043_328
         ),
+    )
+
+    leave = pl.pallas_call(
+        leave_kernel,
+        name="leave",
+        out_shape=(
+            jax.ShapeDtypeStruct((27, 4, 128), F32),
+            jax.ShapeDtypeStruct((3, 6, 6, 384), F32),
+            jax.ShapeDtypeStruct((3,), F32),
+        ),
+        in_specs=[pl.BlockSpec(memory_space=pltpu.VMEM)] * 2 + [pl.BlockSpec(memory_space=pltpu.SMEM)],
+        out_specs=(hbm,) * 2 + (pl.BlockSpec(memory_space=pltpu.SMEM),),
+        scratch_shapes=[dma((2,))],
     )
 
     def on_device(displacement, size_field_modes, velocity):
@@ -894,8 +990,8 @@
             jnp.asarray(wf),
             jnp.asarray(wb),
             jnp.asarray(perm),
-            jnp.asarray(cube),
         )
+        adv, grad, checks = leave(adv, grad, checks)
         return adv.reshape(27, 2, 2, 128), grad, checks
 
     spec = P(None, "gx", "gy", "gz")

time: 66.8 us -> 61.1 us (0.915)
  local copies, waits for them, and re-layouts: 8.1 us -> 0 us
  Pallas kernels: 57.7 us -> 60.4 us
    unnamed x17 -> x0, local copies, waits for them, and re-layouts: 8.03 us -> none
    pallas_call x0 -> x1, Pallas kernels: none -> 2.22 us  [on_device(): adv, grad, checks = leave(adv, grad, checks)]
where the time goes in v2:
time: 61.1 us; the launch traced here: 61 us
  Pallas kernels  60.4 us (99%)
  between operations  0.64 us (1%)
    pallas_call x1, Pallas kernels, on_device(): call(displacement, size_field_modes.reshape(27, 4, 128), velocity.reshape...  58.1 us
    pallas_call x1, Pallas kernels, on_device(): adv, grad, checks = leave(adv, grad, checks)  2.22 us

profile of v2, /device:TPU:1, one launch (start us, length us, event | category | flops | bytes accessed | tf_op | source)
XLA Modules:
  0.0 61.0 jit_solution(15232946247624276786)
XLA Ops:
  0.6 58.1 %tmop_step.1 = (f32[27,4,128]{2,1,0:T(4,128)}, f32[3,6,6,384]{3,2,1,0:T(8,128)}, f32[3]{0:T(128)}) custom-call(f32[3,6,6,384]{3,2,1,0:T(8,128)} %disp_any.1, f32[27,4,128]{2,1,0:T(4,128)} %bitcast.3, f32[3,4,128]{2,1,0:T(4,128)} %bitcast.4, bf16[1536,224]{1,0:T(8,128)(2,1)} %constant.6.clone.wf_any, bf16[448,768]{1,0:T(8,128)(2,1)} %constant.7.clone.wb_any, ...), custom_call_target="tpu_custom_call" | custom-call | tf_op jit(solution)/shard_map/tmop_step/pallas_call | solution.py:986
  58.8 2.2 %leave.1 = (f32[27,4,128]{2,1,0:T(4,128)}, f32[3,6,6,384]{3,2,1,0:T(8,128)}, f32[3]{0:T(128)}) custom-call(f32[27,4,128]{2,1,0:T(4,128)} %get-tuple-element.9.a, f32[3,6,6,384]{3,2,1,0:T(8,128)} %get-tuple-element.10.b, f32[3]{0:T(128)} %get-tuple-element.11.c), custom_call_target="tpu_custom_call" | custom-call | tf_op jit(solution)/shard_map/leave/pallas_call | solution.py:994

commit v3 on v2

--- a/solution.py
+++ b/solution.py
@@ -250,6 +250,21 @@
         zs_out[0, v] = low
         zs_out[1, v] = high
 
+    pl.semaphore_wait(barrier, len(partners))
+
+    def along_z(part, base):
+        return [
+            remote(
+                zs_out.at[w, part], zs_in.at[w, part], z_sem.at[base + w], z_sem.at[base + 2 + w], at(0, 0, to)
+            )
+            for w, to in ((1, 1), (0, -1))
+        ]
+
+    z_field = along_z(pl.ds(0, 2), 0)
+    maxes_a = [
+        remote(max_a.at[0], max_a.at[s], red_sem.at[0, 0, s], red_sem.at[0, 1, s], p)
+        for s, p in group_a
+    ]
     din[...] = jnp.zeros((144, 384), F32)
     loads[5].wait()
     for c in range(3):
@@ -279,16 +294,9 @@
     zs_out[0, 2] = low
     zs_out[1, 2] = high
 
-    pl.semaphore_wait(barrier, len(partners))
-
-    z_up = remote(zs_out.at[1], zs_in.at[1], z_sem.at[0], z_sem.at[1], at(0, 0, 1))
-    z_down = remote(zs_out.at[0], zs_in.at[0], z_sem.at[2], z_sem.at[3], at(0, 0, -1))
-    maxes_a = [
-        remote(max_a.at[0], max_a.at[s], red_sem.at[0, 0, s], red_sem.at[0, 1, s], p)
-        for s, p in group_a
-    ]
-    z_up.wait_recv()
-    z_down.wait_recv()
+    z_nodes = along_z(pl.ds(2, 1), 4)
+    for c in z_field:
+        c.wait_recv()
     for v in range(2):
         from_low = zs_in[1, v]
         from_high = zs_in[0, v]
@@ -408,9 +416,25 @@
 
     def advance(r, hidden):
         src, mid_ref, dst = term.at[2 * r], term.at[2 * r + 1], term.at[2 * r + 2]
+        m = 2 if r == 0 else 1
+        first = outward([take(src, 0, i) for i in range(3)], 0)
+        edge = outward([first[0], first[1], first[2]], 1)
+        values = [edge[0], edge[1], edge[2]] + ([v0, v1] if r == 0 else [])
+        for i, source in enumerate(corner_rows):
+            for w, tile in enumerate(pack_corner(values, source)):
+                diag_out[r, i, w] = tile
+        corner_copies = [
+            remote(
+                diag_out.at[r, i, pl.ds(0, m)],
+                diag_in.at[r, i, pl.ds(0, m)],
+                diag_sem.at[r, 0, i],
+                diag_sem.at[r, 1, i],
+                at(*s),
+            )
+            for i, s in enumerate(corners)
+        ]
         rims = local_rate(src, mid_ref)
         n = 11 if r == 0 else 9
-        m = 2 if r == 0 else 1
         for d in range(2):
             by = 2 - d
             far = outward([take(mid_ref, d, i) for i in range(3)], d)
@@ -423,21 +447,6 @@
                 for w in range(2):
                     face_out[r, 2 * d + w, 9] = v0
                     face_out[r, 2 * d + w, 10] = v1
-        edge = outward([rims[0][0], rims[0][1], rims[0][2]], 1)
-        values = [edge[0], edge[1], edge[2]] + ([v0, v1] if r == 0 else [])
-        for i, source in enumerate(corner_rows):
-            for w, tile in enumerate(pack_corner(values, source)):
-                diag_out[r, i, w] = tile
-        corner_copies = [
-            remote(
-                diag_out.at[r, i, pl.ds(0, m)],
-                diag_in.at[r, i, pl.ds(0, m)],
-                diag_sem.at[r, 0, i],
-                diag_sem.at[r, 1, i],
-                at(*s),
-            )
-            for i, s in enumerate(corners)
-        ]
         copies = [
             remote(
                 face_out.at[r, i, pl.ds(0, n)],
@@ -506,6 +515,27 @@
     later = {}
 
     def hidden0():
+        for c in maxes_a:
+            c.wait_recv()
+        best = max_a[0]
+        for s in range(1, count_a):
+            best = jnp.maximum(best, max_a[s])
+        max_c[0] = best
+        later["pair"] = [
+            remote(max_c.at[0], max_c.at[s], red_sem.at[4, 0, s], red_sem.at[4, 1, s], p)
+            for s, p in group_c
+        ]
+
+    def hidden1():
+        for c in later["pair"]:
+            c.wait_recv()
+        max_b[0] = jnp.maximum(max_c[0], max_c[1])
+        later["max"] = [
+            remote(max_b.at[0], max_b.at[s], red_sem.at[1, 0, s], red_sem.at[1, 1, s], p)
+            for s, p in group_b
+        ]
+        for c in z_nodes:
+            c.wait_recv()
         tx_out[9] = zs_in[0, 2]
         tx_out[10] = zs_in[1, 2]
         for t in range(9):
@@ -522,25 +552,8 @@
             remote(ty_out, ty_in, t_sem.at[0, 1], t_sem.at[1, 1], at(0, -1)),
             remote(td_out, td_in, t_sem.at[0, 2], t_sem.at[1, 2], at(-1, -1)),
         ]
-        for c in maxes_a:
-            c.wait_recv()
-        best = max_a[0]
-        for s in range(1, count_a):
-            best = jnp.maximum(best, max_a[s])
-        max_c[0] = best
-        later["pair"] = [
-            remote(max_c.at[0], max_c.at[s], red_sem.at[4, 0, s], red_sem.at[4, 1, s], p)
-            for s, p in group_c
-        ]
-
-    def hidden1():
-        for c in later["pair"]:
-            c.wait_recv()
-        max_b[0] = jnp.maximum(max_c[0], max_c[1])
-        later["max"] = [
-            remote(max_b.at[0], max_b.at[s], red_sem.at[1, 0, s], red_sem.at[1, 1, s], p)
-            for s, p in group_b
-        ]
+
+    def hidden2():
         for c in later["t"]:
             c.wait_recv()
         for t in range(9):
@@ -576,7 +589,6 @@
             nf[168:224, c * 256 : c * 256 + 128] = jnp.where(wide_lane == 127, b, a)
             nf[168:224, c * 256 + 128 : c * 256 + 256] = jnp.where(wide_lane == 127, a, b)
 
-    def hidden2():
         loads[1].wait()
         for c in range(3):
             a, b = split(nf[:, c * 256 : c * 256 + 256])
@@ -675,14 +687,15 @@
                     gl[rows, c * 256 + tile * 128 : c * 256 + tile * 128 + 128] = lo
         return energy
 
-    energy = lax.fori_loop(0, 16, forces, jnp.zeros((16, 128), F32))
+    energy = lax.fori_loop(0, 16, forces, jnp.zeros((16, 128), F32), unroll=2)
 
     wide_lane = lax.broadcasted_iota(jnp.int32, (56, 128), 1)
     rim = jnp.zeros((56, 128), F32)
     for c in range(3):
         a = gh[:, c * 256 : c * 256 + 256]
         b = gl[:, c * 256 : c * 256 + 256]
-        part = dot(wb_ref[0:224, :], a) + dot(wb_ref[224:448, :], a) + dot(wb_ref[0:224, :], b)
+        both = dot(wb_ref[...], a)
+        part = both[0:224, :] + both[224:448, :] + dot(wb_ref[0:224, :], b)
         r0 = roll(part[168:224, 0:128], 1, 1)
         r1 = roll(part[168:224, 128:256], 1, 1)
         pg[c * 56 : c * 56 + 56, :] = part[0:56, 0:128] + jnp.where(wide_lane == 0, r1, r0)
@@ -748,7 +761,8 @@
             wide_lane == 127, roll(pg[504:560, :], 127 - c, 1), roll(pg[c * 56 : c * 56 + 56, :], 127, 1)
         )
     a, b = split(nt[...])
-    hh[...] = dot(wf_ref[0:768, :], a) + dot(wf_ref[768:1536, :], a) + dot(wf_ref[0:768, :], b)
+    both = dot(wf_ref[...], a)
+    hh[...] = both[0:768, :] + both[768:1536, :] + dot(wf_ref[0:768, :], b)
 
     def coefficients(step, sums):
         col, g = step // 4, step % 4
@@ -782,7 +796,7 @@
         )
 
     none = jnp.zeros((16, 128), F32)
-    sums = lax.fori_loop(0, 16, coefficients, (none, none, none, none))
+    sums = lax.fori_loop(0, 16, coefficients, (none, none, none, none), unroll=2)
     line = lax.broadcasted_iota(jnp.int32, (1, 128), 1)
     values = [energy, square, reach_step] + [total(s) for s in sums]
     mine = jnp.zeros((1, 128), F32)
@@ -871,10 +885,9 @@
 
 def leave_kernel(a, b, c, to_a, to_b, to_c, sem):
     copies = [
-        pltpu.make_async_copy(x, y, sem.at[i]) for i, (x, y) in enumerate(((a, to_a), (b, to_b)))
+        pltpu.make_async_copy(x, y, sem.at[i])
+        for i, (x, y) in enumerate(((a, to_a), (b, to_b), (c, to_c)))
     ]
-    for i in range(3):
-        to_c[i] = c[i]
     for copy in copies:
         copy.start()
     for copy in copies:
@@ -957,7 +970,7 @@
             pltpu.VMEM((2, 1, 128), F32),
             pltpu.VMEM((3, 3, 3, 8, 128), F32),
             dma((8,)),
-            dma((4,)),
+            dma((8,)),
             dma((ROUNDS, 2, 4)),
             dma((ROUNDS, 2, 4)),
             dma((2, 3)),
@@ -977,9 +990,9 @@
             jax.ShapeDtypeStruct((3, 6, 6, 384), F32),
             jax.ShapeDtypeStruct((3,), F32),
         ),
-        in_specs=[pl.BlockSpec(memory_space=pltpu.VMEM)] * 2 + [pl.BlockSpec(memory_space=pltpu.SMEM)],
-        out_specs=(hbm,) * 2 + (pl.BlockSpec(memory_space=pltpu.SMEM),),
-        scratch_shapes=[dma((2,))],
+        in_specs=[pl.BlockSpec(memory_space=pltpu.VMEM)] * 3,
+        out_specs=(hbm,) * 3,
+        scratch_shapes=[dma((3,))],
     )
 
     def on_device(displacement, size_field_modes, velocity):

time: 61.1 us -> 60 us (0.982)
  Pallas kernels: 60.4 us -> 59.2 us
where the time goes in v3:
time: 60 us; the launch traced here: 59.9 us
  Pallas kernels  59.2 us (99%)
  between operations  0.64 us (1%)
    pallas_call x1, Pallas kernels, on_device(): call(displacement, size_field_modes.reshape(27, 4, 128), velocity.reshape...  57.6 us
    pallas_call x1, Pallas kernels, on_device(): adv, grad, checks = leave(adv, grad, checks)  1.67 us

profile of v3, /device:TPU:1, one launch (start us, length us, event | category | flops | bytes accessed | tf_op | source)
XLA Modules:
  0.0 59.9 jit_solution(147362540749518360)
XLA Ops:
  0.6 57.6 %tmop_step.1 = (f32[27,4,128]{2,1,0:T(4,128)}, f32[3,6,6,384]{3,2,1,0:T(8,128)}, f32[3]{0:T(128)}) custom-call(f32[3,6,6,384]{3,2,1,0:T(8,128)} %disp_any.1, f32[27,4,128]{2,1,0:T(4,128)} %bitcast.3, f32[3,4,128]{2,1,0:T(4,128)} %bitcast.4, bf16[1536,224]{1,0:T(8,128)(2,1)} %constant.6.clone.wf_any, bf16[448,768]{1,0:T(8,128)(2,1)} %constant.7.clone.wb_any, ...), custom_call_target="tpu_custom_call" | custom-call | tf_op jit(solution)/shard_map/tmop_step/pallas_call | solution.py:999
  58.2 1.7 %leave.1 = (f32[27,4,128]{2,1,0:T(4,128)}, f32[3,6,6,384]{3,2,1,0:T(8,128)}, f32[3]{0:T(128)}) custom-call(f32[27,4,128]{2,1,0:T(4,128)} %get-tuple-element.9.a, f32[3,6,6,384]{3,2,1,0:T(8,128)} %get-tuple-element.10.b, f32[3]{0:T(128)} %get-tuple-element.11.c), custom_call_target="tpu_custom_call" | custom-call | tf_op jit(solution)/shard_map/leave/pallas_call | solution.py:1007
